TPU v7x, 128 devices: a whole 4x4x4 slice. The times are simulated.
128 devices in a mesh: dp: 1, ey: 16 (over z, y), ex: 8 (over x, core).
Axes of the slice: x: 4, y: 4, z: 4, core: 2. Of those that a mesh axis runs over, the one named last changes fastest.
Arguments:
- x: bfloat16 [32768, 2048], P(('dp', 'ey', 'ex'))
- ids: int32 [32768, 8], P(('dp', 'ey', 'ex'))
- gates: float32 [32768, 8], P(('dp', 'ey', 'ex'))
- w1: bfloat16 [128, 2048, 768], P(('ey', 'ex'))
- w3: bfloat16 [128, 2048, 768], P(('ey', 'ex'))
- w2: bfloat16 [128, 768, 2048], P(('ey', 'ex'))
Outputs:
- output: bfloat16 [32768, 2048], P(('dp', 'ey', 'ex'))
All inputs are finite; a program needn't handle non-finite values.
Results may differ from a plain program's by a relative error of at most 0.001.
Values are sent between devices in bfloat16 or wider.
A program may use at most 1 GiB of HBM per device.

v0:
```python
import jax
import jax.numpy as jnp
from jax import lax
from jax.sharding import PartitionSpec as P

CAPF = 2


def solution(mesh):
    nx = mesh.shape["ex"]
    nd = mesh.shape["ey"] * nx
    axes = ("ey", "ex")
    tok = P(("dp", "ey", "ex"), None)
    wsp = P(("ey", "ex"), None, None)

    def local(x, ids, gates, w1, w3, w2):
        t, hd = x.shape
        top = ids.shape[1]
        el = w1.shape[0]
        cap = min(t, CAPF * t * top // nd)
        me = lax.axis_index("ey") * nx + lax.axis_index("ex")
        dev = ids // el
        hit = jnp.any(dev[:, :, None] == jnp.arange(nd)[None, None, :], axis=1)
        rank = jnp.cumsum(hit.astype(jnp.int32), axis=0) - 1
        kept = hit & (rank < cap)
        slot = jnp.where(kept, rank, cap)
        dst = jnp.broadcast_to(jnp.arange(nd)[None, :], (t, nd))
        src = jnp.broadcast_to(jnp.arange(t)[:, None], (t, nd))
        sx = jnp.zeros((nd, cap, hd), x.dtype).at[dst, slot].set(x[src], mode="drop")
        si = jnp.full((nd, cap, top), -1, jnp.int32).at[dst, slot].set(ids[src], mode="drop")
        sg = jnp.zeros((nd, cap, top), jnp.float32).at[dst, slot].set(gates[src], mode="drop")
        rx = lax.all_to_all(sx, axes, 0, 0, tiled=True).reshape(nd * cap, hd)
        ri = lax.all_to_all(si, axes, 0, 0, tiled=True).reshape(nd * cap, top)
        rg = lax.all_to_all(sg, axes, 0, 0, tiled=True).reshape(nd * cap, top)
        a1 = jnp.einsum("rh,ehf->erf", rx, w1, preferred_element_type=jnp.float32)
        a3 = jnp.einsum("rh,ehf->erf", rx, w3, preferred_element_type=jnp.float32)
        hh = (jax.nn.silu(a1) * a3).astype(jnp.bfloat16)
        o = jnp.einsum("erf,efh->erh", hh, w2, preferred_element_type=jnp.float32).astype(jnp.bfloat16)
        eid = me * el + jnp.arange(el)
        coef = jnp.sum(jnp.where(ri[None, :, :] == eid[:, None, None], rg[None, :, :], 0.0), axis=2)
        part = jnp.sum(coef[:, :, None] * o, axis=0).reshape(nd, cap, hd)
        back = lax.all_to_all(part, axes, 0, 0, tiled=True)
        got = back[dst, jnp.minimum(slot, cap - 1)]
        moe_out = jnp.sum(jnp.where(kept[:, :, None], got, 0.0), axis=1)
        return (x.astype(jnp.float32) + moe_out).astype(jnp.bfloat16)

    return jax.shard_map(local, mesh=mesh, in_specs=(tok, tok, tok, wsp, wsp, wsp),
                         out_specs=tok, check_vma=False)
```

profile of v0, /device:TPU:1, one launch (start us, length us, event | category | flops | bytes accessed | tf_op | source)
XLA Modules:
  0.0 3530.0 jit_solution(17084262393561383212)
XLA Ops:
  0.0 0.6 bitcast_clamp_fusion
  0.7 1.2 copy.36
  2.6 0.8 and_reduce_fusion
  3.4 1.4 multiply_reduce_fusion
  4.8 1.5 copy.42
  6.3 1.6 select_bitcast_fusion
  7.9 482.3 %scatter_custom_fusion.1 = f32[4096,8]{1,0:T(8,128)} fusion(s32[32768]{0:T(1024)} %select_bitcast_fusion, f32[256,8]{1,0:T(8,128)} %copy.42, s32[32768]{0:T(1024)} %bitcast_clamp_fusion, f32[]{:T(128)} %constant.46.clone.1), kind=kCustom, calls=%fused_computation.11 | custom fusion | bytes 131584
  490.2 3.0 copy.44
  493.2 1.9 reshape.173
  495.1 12.0 all-to-all-start.1
  507.1 194.4 %scatter_custom_fusion = s32[4096,8]{1,0:T(8,128)} fusion(s32[32768]{0:T(1024)} %select_bitcast_fusion, s32[256,8]{1,0:T(8,128)S(1)} %copy.36, s32[32768]{0:T(1024)} %bitcast_clamp_fusion, s32[]{:T(128)} %constant.21.clone.1), kind=kCustom, calls=%fused_computation.13 | custom fusion | bytes 131584
  701.5 3.0 copy.41
  704.4 1.9 reshape.175
  706.4 10.1 all-to-all-start
  716.5 1084.2 %scatter_custom_fusion.2 = bf16[4096,2048]{1,0:T(8,128)(2,1)} fusion(s32[32768]{0:T(1024)} %select_bitcast_fusion, bf16[256,2048]{1,0:T(8,128)(2,1)} %param.6, s32[32768]{0:T(1024)} %bitcast_clamp_fusion, bf16[]{:T(256)} %constant.47.clone.1), kind=kCustom, calls=%fused_computation.8 | custom fusion | bytes 16777728
  1800.7 0.6 copy-done.2
  1801.4 10.2 all-to-all-start.2
  1811.6 0.5 broadcast.157
  1812.1 1.8 reduce.10
  1813.9 1.0 reshape.174
  1815.4 1.8 reduce.9
  1817.1 1.0 reshape.176
  1818.1 1.4 select_reduce_fusion.1
  1819.6 221.8 %all-to-all-done.2 = bf16[128,32,2048]{2,1,0:T(8,128)(2,1)} async-done(((bf16[128,32,2048]{2,1,0:T(8,128)(2,1)}), bf16[128,32,2048]{2,1,0:T(8,128)(2,1)}, u32[]{:S(2)}, u32[]{:S(2)}) %all-to-all-start.2) | async-done | bytes 16777248 | tf_op jit(solution)/shard_map/all_to_all | solution.py:32
  2041.4 19.2 fusion.15
  2060.6 37.8 %convert_multiply_fusion = f32[4096,2048]{1,0:T(8,128)} fusion(f32[4096]{0:T(1024)S(1)} %mul.22, f32[4096,768]{1,0:T(8,128)} %fusion.15, bf16[4096,2048]{1,0:T(8,128)(2,1)} %bitcast.12, bf16[1,768,2048]{2,1,0:T(8,128)(2,1)S(1)} %copy-done, bf16[1,2048,768]{2,1,0:T(8,128)(2,1)} %param.10), kind=kOutput, calls=%fused_computation.10 | convolution fusion | flops 25813843968 | bytes 69222400 | tf_op jit(solution)/shard_map/erf,efh->erh/dot_general | solution.py:38
  2098.4 28.4 all-to-all-start.3
  2126.8 0.6 fusion.28
  2127.6 499.9 %all-to-all-done.3 = f32[128,32,2048]{2,1,0:T(8,128)} async-done(((f32[128,32,2048]{2,1,0:T(8,128)}), f32[128,32,2048]{2,1,0:T(8,128)}, u32[]{:S(2)}, u32[]{:S(2)}) %all-to-all-start.3) | async-done | bytes 33554464 | tf_op jit(solution)/shard_map/all_to_all | solution.py:42
  2627.5 817.5 %gather_fusion = f32[32768,2048]{1,0:T(8,128)} fusion(f32[128,32,2048]{2,1,0:T(8,128)} %all-to-all-done.3, s32[32768]{0:T(1024)S(1)} %fusion.25), kind=kCustom, calls=%fused_computation.3 | custom fusion | bytes 537133056 | tf_op jit(solution)/shard_map/gather | solution.py:43
  3444.9 81.7 %select_reduce_fusion = f32[256,2048]{1,0:T(8,128)} fusion(pred[256,128]{1,0:T(8,128)(4,1)S(1)} %copy-done.3, f32[32768,2048]{1,0:T(8,128)} %gather_fusion), kind=kLoop, calls=%fused_computation.7 | loop fusion | flops 133693440 | bytes 270565376 | tf_op jit(solution)/shard_map/reduce_sum | solution.py:44
  3526.7 3.1 add_convert_fusion
  (22 shorter events, 1.4 us)
Async XLA Ops:
  0.0 2060.6 %copy-start = (bf16[1,768,2048]{2,1,0:T(8,128)(2,1)S(1)}, bf16[1,768,2048]{2,1,0:T(8,128)(2,1)}, u32[]{:S(2)}) copy-start(bf16[1,768,2048]{2,1,0:T(8,128)(2,1)} %param.11) | copy-start | bytes 9437188
  495.1 211.3 %all-to-all-start.1 = ((f32[128,1,256]{2,1,0:T(1,128)}), f32[128,1,256]{2,1,0:T(1,128)}, u32[]{:S(2)}, u32[]{:S(2)}) async-start(f32[128,1,256]{2,1,0:T(1,128)} %reshape.173), calls=%async_computation.1 | async-start | bytes 262144 | tf_op jit(solution)/shard_map/all_to_all | solution.py:34
  706.4 1094.3 %all-to-all-start = ((s32[128,1,256]{2,1,0:T(1,128)}), s32[128,1,256]{2,1,0:T(1,128)S(1)}, u32[]{:S(2)}, u32[]{:S(2)}) async-start(s32[128,1,256]{2,1,0:T(1,128)} %reshape.175), calls=%async_computation | async-start | bytes 262144 | tf_op jit(solution)/shard_map/all_to_all | solution.py:33
  1800.7 0.7 copy-start.2
  1801.4 240.0 %all-to-all-start.2 = ((bf16[128,32,2048]{2,1,0:T(8,128)(2,1)}), bf16[128,32,2048]{2,1,0:T(8,128)(2,1)}, u32[]{:S(2)}, u32[]{:S(2)}) async-start(bf16[128,32,2048]{2,1,0:T(8,128)(2,1)} %bitcast.98), calls=%async_computation.2 | async-start | bytes 33554432 | tf_op jit(solution)/shard_map/all_to_all | solution.py:32
  2098.4 529.1 %all-to-all-start.3 = ((f32[128,32,2048]{2,1,0:T(8,128)}), f32[128,32,2048]{2,1,0:T(8,128)}, u32[]{:S(2)}, u32[]{:S(2)}) async-start(f32[128,32,2048]{2,1,0:T(8,128)} %bitcast.99), calls=%async_computation.3 | async-start | bytes 67108864 | tf_op jit(solution)/shard_map/all_to_all | solution.py:42
  2627.5 817.5 %copy-start.3 = (pred[256,128]{1,0:T(8,128)(4,1)S(1)}, pred[256,128]{1,0:T(8,128)(4,1)}, u32[]{:S(2)}) copy-start(pred[256,128]{1,0:T(8,128)(4,1)} %fusion.28) | copy-start | bytes 98308
  3444.9 84.8 %copy-start.1 = (bf16[1,768,2048]{2,1,0:T(8,128)(2,1)S(1)}, bf16[1,768,2048]{2,1,0:T(8,128)(2,1)}, u32[]{:S(2)}) copy-start(bf16[1,768,2048]{2,1,0:T(8,128)(2,1)} %param.11) | copy-start | bytes 9437188
where the time goes:
time: 3580 us; the launch traced here: 3530 us
  local copies, waits for them, and re-layouts  2590 us (72%)
  waiting for transfers between devices  722 us (20%)
  other arithmetic  95.6 us (3%)
  starting transfers between devices  60.7 us (2%)
  matrix products  57 us (2%)
    unnamed x17, local copies, waits for them, and re-layouts  1770 us
    gather x1, local copies, waits for them, and re-layouts, local(): got = back[dst, jnp.minimum(slot, cap - 1)]  817 us
    all_to_all x1, waiting for transfers between devices, local(): back = lax.all_to_all(part, axes, 0, 0, tiled=True)  500 us
    all_to_all x1, waiting for transfers between devices, local(): rx = lax.all_to_all(sx, axes, 0, 0, tiled=True).reshape(nd * cap, hd)  222 us
    reduce_sum x1, other arithmetic, local(): moe_out = jnp.sum(jnp.where(kept[:, :, None], got, 0.0), axis=1)  81.7 us
  transfers between devices with their start and end apart: 4, of which 2 were waited for; matrix products, arithmetic and copies ran while one was open for 37% of the time, Pallas kernels for 0%

commit v1 on v0

v1 whole, which is shorter than its diff:
```python
import jax
import jax.numpy as jnp
from jax import lax
from jax.sharding import PartitionSpec as P

CAPF = 2
FULL = 16384.0


def solution(mesh):
    nx = mesh.shape["ex"]
    nd = mesh.shape["ey"] * nx
    axes = ("ey", "ex")
    tok = P(("dp", "ey", "ex"), None)
    wsp = P(("ey", "ex"), None, None)
    bf16, f16, f32 = jnp.bfloat16, jnp.float16, jnp.float32

    def top8(v):
        return lax.reduce_precision(jnp.minimum(v, float(jnp.finfo(bf16).max)), 8, 7)

    def split3(v):
        a = top8(v)
        b = top8(v - a)
        c = top8(v - a - b)
        return a.astype(bf16), b.astype(bf16), c.astype(bf16)

    def local(x, ids, gates, w1, w3, w2):
        t, hd = x.shape
        top = ids.shape[1]
        cap = min(t, CAPF * t * top // nd)
        match = ids[:, :, None] == jnp.arange(nd)[None, None, :]
        hit = jnp.any(match, axis=1)
        gate = jnp.sum(jnp.where(match, gates[:, :, None], 0.0), axis=1)
        lower = (jnp.arange(t)[:, None] >= jnp.arange(t)[None, :]).astype(bf16)
        rank = jnp.dot(lower, hit.astype(bf16), preferred_element_type=f32).astype(jnp.int32) - 1
        slot = jnp.where(hit & (rank < cap), rank, cap)

        sel = slot.T[:, None, :] == jnp.arange(cap)[None, :, None]
        send = jnp.dot(sel.astype(bf16).reshape(nd * cap, t), x,
                       preferred_element_type=f32).astype(bf16)
        rx = lax.all_to_all(send.reshape(nd, cap, hd), axes, 0, 0, tiled=True).reshape(nd * cap, hd)

        a1 = jnp.dot(rx, w1[0], preferred_element_type=f32)
        a3 = jnp.dot(rx, w3[0], preferred_element_type=f32)
        hh = (jax.nn.silu(a1) * a3).astype(bf16)
        o = jnp.dot(hh, w2[0], preferred_element_type=f32)
        peak = jnp.maximum(jnp.max(jnp.abs(o), axis=1), 1e-34)
        o = (o * (FULL / peak)[:, None]).astype(f16)
        back = lax.all_to_all(o.reshape(nd, cap, hd), axes, 0, 0, tiled=True).reshape(nd * cap, hd)
        peak = lax.all_to_all(peak.reshape(nd, cap), axes, 0, 0, tiled=True).reshape(1, nd * cap)

        grow = (jnp.arange(nd)[:, None] == (jnp.arange(nd * cap) // cap)[None, :]).astype(bf16)
        wide = lambda v: jnp.dot(v, grow, preferred_element_type=f32)
        mine = wide(slot.astype(bf16)) == (jnp.arange(nd * cap) % cap).astype(f32)[None, :]
        g = sum(wide(part) for part in split3(gate))
        wt = jnp.concatenate(split3(jnp.where(mine, g * (peak * (1.0 / FULL)), 0.0)), axis=0)
        wt = lax.optimization_barrier(wt)
        back = back.astype(f32)
        hi = top8(back)
        hi, lo = hi.astype(bf16), (back - hi).astype(bf16)
        acc = jnp.dot(wt, hi, preferred_element_type=f32) + jnp.dot(wt, lo, preferred_element_type=f32)
        moe = acc[:t] + acc[t:2 * t] + acc[2 * t:]
        return (x.astype(f32) + moe).astype(bf16)

    return jax.shard_map(local, mesh=mesh, in_specs=(tok, tok, tok, wsp, wsp, wsp),
                         out_specs=tok, check_vma=False)
```

time: 3580 us -> 647 us (0.18)
  the two profiles are of different devices: /device:TPU:1 before, /device:TPU:37 now
where the time goes in v1:
time: 647 us; the launch traced here: 642 us
  blocking collectives  231 us (36%)
  waiting for transfers between devices  226 us (35%)
  matrix products  120 us (19%)
  other arithmetic  35.5 us (5%)
  starting transfers between devices  20.7 us (3%)
  local copies, waits for them, and re-layouts  8.39 us (1%)
    all_to_all x1, blocking collectives, local(): lax.all_to_all(send.reshape(nd, cap, hd), axes, 0, 0, tiled=True)  231 us
    all_to_all x1, waiting for transfers between devices, local(): lax.all_to_all(o.reshape(nd, cap, hd), axes, 0, 0, tiled=True)  226 us
    dot_general x1, matrix products, local(): o = jnp.dot(hh, w2[0], preferred_element_type=f32)  38 us
    dot_general x1, matrix products, local(): jnp.dot(wt, lo, preferred_element_type=f32)  22.7 us
    dot_general x1, matrix products, local(): jnp.dot(wt, hi, preferred_element_type=f32)  19.6 us
    convert_element_type x1, other arithmetic, local(): o = (o * (FULL / peak)[:, None]).astype(f16)  18.1 us
    dot_general x1, matrix products, local(): a1 = jnp.dot(rx, w1[0], preferred_element_type=f32)  16.6 us
  transfers between devices with their start and end apart: 2, of which 1 were waited for; matrix products, arithmetic and copies ran while one was open for 6% of the time, Pallas kernels for 0%

profile of v1, /device:TPU:37, one launch (start us, length us, event | category | flops | bytes accessed | tf_op | source)
XLA Modules:
  0.0 641.6 jit_solution(3918679419313329602)
XLA Ops:
  0.0 0.0 copy-start
  0.0 1.0 copy.17
  1.0 0.4 fusion.31
  1.4 0.6 copy-done.5
  2.0 0.8 bitcast_select_fusion
  2.9 0.1 eq.85
  3.0 0.1 copy.19
  3.1 1.5 bitcast_compare_fusion
  4.6 11.8 %convolution_convert_fusion = bf16[4096,2048]{1,0:T(8,128)(2,1)} fusion(pred[4096,256]{1,0:T(32,128)(4,1)} %bitcast_compare_fusion, bf16[256,2048]{1,0:T(8,128)(2,1)} %param.6), kind=kOutput, calls=%fused_computation.11 | convolution fusion | flops 4303355904 | bytes 18874368 | tf_op jit(solution)/shard_map/dot_general | solution.py:39
  16.4 230.5 %all_to_all.16 = bf16[128,32,2048]{2,1,0:T(8,128)(2,1)S(1)} all-to-all(bf16[128,32,2048]{2,1,0:T(8,128)(2,1)} %bitcast.38), channel_id=1, replica_groups=mesh['dp'=1,'ey'=16,'ex'=8] {'ey','ex'}, dimensions={0} | all-to-all | bytes 33554432 | tf_op jit(solution)/shard_map/all_to_all | solution.py:41
  246.9 5.7 copy-done.2
  252.6 16.6 %fusion.21 = f32[4096,768]{1,0:T(8,128)} fusion(bf16[4096,2048]{1,0:T(8,128)(2,1)S(1)} %bitcast.40, bf16[1,2048,768]{2,1,0:T(8,128)(2,1)S(1)} %copy-done.8), kind=kOutput, calls=%fused_computation.30 | convolution fusion | flops 12884901888 | bytes 32505856 | tf_op jit(solution)/shard_map/dot_general | solution.py:43
  269.2 38.0 %abs_reduce_fusion = (f32[4096]{0:T(1024)S(1)}, f32[4096,2048]{1,0:T(8,128)}) fusion(bf16[1,768,2048]{2,1,0:T(8,128)(2,1)S(1)} %copy-done, f32[4096,768]{1,0:T(8,128)} %fusion.21, bf16[4096,2048]{1,0:T(8,128)(2,1)} %bitcast.41, bf16[1,2048,768]{2,1,0:T(8,128)(2,1)} %param.10), kind=kOutput, calls=%fused_computation.6 | convolution fusion | flops 25805451264 | bytes 69222400 | tf_op jit(solution)/shard_map/dot_general | solution.py:46
  307.2 0.7 max.23
  307.9 10.1 %all-to-all-start.1 = ((f32[128,1,32]{2,1,0:T(1,128)}), f32[128,1,32]{2,1,0:T(1,128)S(1)}, u32[]{:S(2)}, u32[]{:S(2)}) async-start(f32[128,1,32]{2,1,0:T(1,128)} %bitcast.8), calls=%async_computation.1 | async-start | bytes 131072 | tf_op jit(solution)/shard_map/all_to_all | solution.py:50
  318.0 18.1 %multiply_convert_fusion = f16[4096,2048]{1,0:T(8,128)(2,1)} fusion(f32[4096,2048]{1,0:T(8,128)} %get-tuple-element.13, f32[4096]{0:T(1024)S(1)} %get-tuple-element.8), kind=kLoop, calls=%fused_computation.5 | loop fusion | flops 16777216 | bytes 50348032 | tf_op jit(solution)/shard_map/convert_element_type | solution.py:48
  336.1 0.0 all-to-all-done.1
  336.1 10.6 %all-to-all-start.2 = ((f16[128,32,2048]{2,1,0:T(8,128)(2,1)}), f16[128,32,2048]{2,1,0:T(8,128)(2,1)}, u32[]{:S(2)}, u32[]{:S(2)}) async-start(f16[128,32,2048]{2,1,0:T(8,128)(2,1)} %bitcast.39), calls=%async_computation.2 | async-start | bytes 33554432 | tf_op jit(solution)/shard_map/all_to_all | solution.py:49
  346.7 0.1 copy.18
  346.9 1.3 select_reduce_fusion
  348.1 0.7 fusion.25
  348.9 2.0 convolution_compare_fusion
  351.0 2.7 convolution_add_fusion.1
  353.7 0.2 multiply_reduce_fusion
  353.8 0.1 mul.41
  353.9 4.9 fusion.14
  358.8 9.4 %pad_maximum_fusion = bf16[768,4096]{1,0:T(8,128)(2,1)} fusion(bf16[256,4096]{1,0:T(8,128)(2,1)S(1)} %get-tuple-element.6, bf16[256,4096]{1,0:T(8,128)(2,1)S(1)} %get-tuple-element.7, bf16[256,4096]{1,0:T(8,128)(2,1)S(1)} %get-tuple-element.5), kind=kLoop, calls=%fused_computation.13 | loop fusion | flops 18874368 | bytes 12582912 | tf_op jit(solution)/shard_map/concatenate | solution.py:56
  368.2 226.1 %all-to-all-done.2 = f16[128,32,2048]{2,1,0:T(8,128)(2,1)} async-done(((f16[128,32,2048]{2,1,0:T(8,128)(2,1)}), f16[128,32,2048]{2,1,0:T(8,128)(2,1)}, u32[]{:S(2)}, u32[]{:S(2)}) %all-to-all-start.2) | async-done | bytes 16777248 | tf_op jit(solution)/shard_map/all_to_all | solution.py:49
  594.3 22.7 %fusion.3 = f32[768,2048]{1,0:T(8,128)} fusion(bf16[768,4096]{1,0:T(8,128)(2,1)} %pad_maximum_fusion, f16[4096,2048]{1,0:T(8,128)(2,1)} %bitcast.11), kind=kOutput, calls=%fused_computation.7 | convolution fusion | flops 12926844928 | bytes 29360128 | tf_op jit(solution)/shard_map/dot_general | solution.py:61
  617.0 0.0 copy-done.3
  617.0 19.6 %fusion.15 = f32[768,2048]{1,0:T(8,128)} fusion(f32[768,2048]{1,0:T(8,128)} %fusion.3, bf16[768,4096]{1,0:T(8,128)(2,1)S(1)} %copy-done.3, f16[4096,2048]{1,0:T(8,128)(2,1)} %bitcast.11), kind=kOutput, calls=%fused_computation.27 | convolution fusion | flops 12920029184 | bytes 35651584 | tf_op jit(solution)/shard_map/dot_general | solution.py:61
  636.6 4.6 fusion.24
  (19 shorter events, 0.1 us)
Async XLA Ops:
  0.0 269.2 %copy-start = (bf16[1,768,2048]{2,1,0:T(8,128)(2,1)S(1)}, bf16[1,768,2048]{2,1,0:T(8,128)(2,1)}, u32[]{:S(2)}) copy-start(bf16[1,768,2048]{2,1,0:T(8,128)(2,1)} %param.11) | copy-start | bytes 9437188
  1.4 0.6 copy-start.5
  16.4 236.2 %copy-start.8 = (bf16[1,2048,768]{2,1,0:T(8,128)(2,1)S(1)}, bf16[1,2048,768]{2,1,0:T(8,128)(2,1)}, u32[]{:S(2)}) copy-start(bf16[1,2048,768]{2,1,0:T(8,128)(2,1)} %param.9) | copy-start | bytes 9437188
  246.9 5.7 copy-start.2
  307.9 28.1 %all-to-all-start.1 = ((f32[128,1,32]{2,1,0:T(1,128)}), f32[128,1,32]{2,1,0:T(1,128)S(1)}, u32[]{:S(2)}, u32[]{:S(2)}) async-start(f32[128,1,32]{2,1,0:T(1,128)} %bitcast.8), calls=%async_computation.1 | async-start | bytes 131072 | tf_op jit(solution)/shard_map/all_to_all | solution.py:50
  336.1 10.7 %copy-start.7 = (f32[256,8]{0,1:T(8,128)S(1)}, f32[256,8]{0,1:T(8,128)}, u32[]{:S(2)}) copy-start(f32[256,8]{0,1:T(8,128)} %param.8) | copy-start | bytes 24580
  336.1 12.8 %copy-start.6 = (pred[256,128]{1,0:T(8,128)(4,1)S(1)}, pred[256,128]{1,0:T(8,128)(4,1)}, u32[]{:S(2)}) copy-start(pred[256,128]{1,0:T(8,128)(4,1)} %copy-done.5) | copy-start | bytes 98308
  336.1 12.8 %copy-start.9 = (s32[256,128]{1,0:T(8,128)S(1)}, s32[256,128]{1,0:T(8,128)}, u32[]{:S(2)}) copy-start(s32[256,128]{1,0:T(8,128)} %get-tuple-element.11) | copy-start | bytes 393220
  336.1 258.2 %all-to-all-start.2 = ((f16[128,32,2048]{2,1,0:T(8,128)(2,1)}), f16[128,32,2048]{2,1,0:T(8,128)(2,1)}, u32[]{:S(2)}, u32[]{:S(2)}) async-start(f16[128,32,2048]{2,1,0:T(8,128)(2,1)} %bitcast.39), calls=%async_computation.2 | async-start | bytes 33554432 | tf_op jit(solution)/shard_map/all_to_all | solution.py:49
  594.3 22.7 %copy-start.3 = (bf16[768,4096]{1,0:T(8,128)(2,1)S(1)}, bf16[768,4096]{1,0:T(8,128)(2,1)}, u32[]{:S(2)}) copy-start(bf16[768,4096]{1,0:T(8,128)(2,1)} %pad_maximum_fusion) | copy-start | bytes 18874372
  617.0 19.6 %copy-start.4 = (bf16[256,2048]{1,0:T(8,128)(2,1)S(1)}, bf16[256,2048]{1,0:T(8,128)(2,1)}, u32[]{:S(2)}) copy-start(bf16[256,2048]{1,0:T(8,128)(2,1)} %param.6) | copy-start | bytes 3145732
  617.0 24.2 %copy-start.1 = (bf16[1,768,2048]{2,1,0:T(8,128)(2,1)S(1)}, bf16[1,768,2048]{2,1,0:T(8,128)(2,1)}, u32[]{:S(2)}) copy-start(bf16[1,768,2048]{2,1,0:T(8,128)(2,1)} %param.11) | copy-start | bytes 9437188

commit v2 on v1

v2 whole, which is shorter than its diff:
```python
import functools

import jax
import jax.numpy as jnp
from jax import lax
from jax.experimental import pallas as pl
from jax.experimental.pallas import tpu as pltpu
from jax.sharding import PartitionSpec as P

CAPF = 2
FULL = 16384.0
RING = 4
CORES = 2
PARTS = 2
IDROWS = 8
ORDERS = ((0, 1, 2), (2, 0, 1), (1, 2, 0))
bf16, f16, f32 = jnp.bfloat16, jnp.float16, jnp.float32


def column_groups(hd):
    tiles = hd // 128
    first = -(-tiles // 3)
    second = -(-(tiles - first) // 2)
    widths = [first * 128, second * 128, (tiles - first - second) * 128]
    starts = [0, widths[0], widths[0] + widths[1]]
    return list(zip(starts, widths))


def dispatch_kernel(t, cap, groups, x_ref, rx_ref, got, out, upper, pick, load_sem, gsend, grecv, rsend, rrecv, self_sem):
    ey, ex, dp = lax.axis_index("ey"), lax.axis_index("ex"), lax.axis_index("dp")
    me = [ey // RING, ey % RING, ex // CORES]
    core = ex % CORES
    half = cap // PARTS
    rows = t + IDROWS
    split = (rows // 2 + 7) // 8 * 8

    def device(coords, c):
        return (dp, coords[0] * RING + coords[1], coords[2] * CORES + c)

    def shifted(axis, by, c=None):
        coords = list(me)
        coords[axis] = (coords[axis] + by) % RING
        return device(coords, core if c is None else c)

    loads = []
    for g, (start, width) in enumerate(groups):
        loads.append(pltpu.make_async_copy(
            x_ref.at[:, pl.ds(start, width)], got.at[g, 0, 0, :, pl.ds(0, width)], load_sem.at[g]))
        loads[-1].start()

    barrier = pltpu.get_barrier_semaphore()
    peers = [(axis, by, dc) for axis in range(3) for by in range(1, RING) for dc in range(CORES)] + [(0, 0, 1)]
    for axis, by, dc in peers:
        pl.semaphore_signal(barrier, inc=1, device_id=shifted(axis, by, (core + dc) % CORES),
                            device_id_type=pl.DeviceIdType.MESH)
    row = lax.broadcasted_iota(jnp.int32, (t, t), 0)
    col = lax.broadcasted_iota(jnp.int32, (t, t), 1)
    upper[...] = jnp.where(row <= col, 1.0, 0.0).astype(bf16)
    pl.semaphore_wait(barrier, len(peers))
    for load in loads:
        load.wait()

    def hop(g, index, block, to, axis, by, part=None):
        width = groups[g][1]
        at = pl.ds(0, rows) if part is None else part
        copy = pltpu.make_async_remote_copy(
            src_ref=got.at[g, block[0], block[1], at, pl.ds(0, width)],
            dst_ref=got.at[g, to[0], to[1], at, pl.ds(0, width)],
            send_sem=gsend.at[g, index], recv_sem=grecv.at[g, index],
            device_id=shifted(axis, by), device_id_type=pl.DeviceIdType.MESH)
        copy.start()
        hops[g, index] = copy

    hops = {}
    low, high = pl.ds(0, split), pl.ds(split, rows - split)

    def first(g):
        p = ORDERS[g][0]
        hop(g, 0, (0, 0), (3, 0), p, 1)
        hop(g, 1, (0, 0), (1, 0), p, 3)

    def second(g, i):
        q = ORDERS[g][1]
        hop(g, 4 + 4 * i, (i, 0), (i, 3), q, 1)
        hop(g, 5 + 4 * i, (i, 0), (i, 1), q, 3)

    def second_on(g, i):
        q = ORDERS[g][1]
        hops[g, 4 + 4 * i].wait_recv()
        hop(g, 6 + 4 * i, (i, 3), (i, 2), q, 1, low)
        hops[g, 5 + 4 * i].wait_recv()
        hop(g, 7 + 4 * i, (i, 1), (i, 2), q, 3, high)

    everyone = range(len(groups))
    for g in everyone:
        first(g)
        second(g, 0)
    for g in everyone:
        p = ORDERS[g][0]
        hops[g, 0].wait_recv()
        hop(g, 2, (3, 0), (2, 0), p, 1, low)
        second(g, 3)
        hops[g, 1].wait_recv()
        hop(g, 3, (1, 0), (2, 0), p, 3, high)
        second(g, 1)
    for g in everyone:
        second_on(g, 0)
    for g in everyone:
        hops[g, 2].wait_recv()
        hops[g, 3].wait_recv()
        second(g, 2)

    def choose(g, j):
        p, _, r = ORDERS[g]
        width = groups[g][1]
        stride = (RING * RING * CORES, RING * CORES, CORES)[r]
        base = ey * (RING * CORES) + ex - core - me[r] * stride

        def one(i, _):
            ids = got[g, i, j, pl.ds(t, IDROWS), pl.ds(0, t)].astype(f32)
            lines = []
            for k in range(RING * CORES):
                expert = (base + (k // CORES) * stride + k % CORES).astype(f32)
                lines.append(jnp.sum(jnp.where(ids == expert, 1.0, 0.0), axis=0, keepdims=True))
            hit = jnp.concatenate(lines, axis=0)
            rank = jnp.dot(hit.astype(bf16), upper[...], preferred_element_type=f32)
            slot = jnp.where((hit > 0.5) & (rank < cap + 0.5), rank - 1.0, -1.0)
            wanted = lax.broadcasted_iota(jnp.int32, (cap, t), 0).astype(f32)
            for k in range(RING * CORES):
                pick[pl.ds(k * cap, cap), :] = jnp.where(slot[k:k + 1, :] == wanted, 1.0, 0.0).astype(bf16)
            place = (me[p] + i) % RING

            def tile(n, _):
                at = pl.ds(pl.multiple_of(n * 128, 128), 128)
                val = jnp.dot(pick[...], got[g, i, j, pl.ds(0, t), at], preferred_element_type=f32).astype(bf16)
                for k in range(RING * CORES):
                    for h in range(PARTS):
                        begin = k * cap + h * half
                        out[g, j, k, h, place, :, at] = val[begin:begin + half]
                return 0

            return lax.fori_loop(0, width // 128, tile, 0)

        lax.fori_loop(0, RING, one, 0)

    def place_in(ref, g, j):
        start, width = groups[g]
        p, q, r = ORDERS[g]
        at = [None, None, None]
        at[p] = slice(None)
        at[q] = (me[q] + j) % RING
        at[r] = me[r]
        return ref.at[:, at[0], at[1], at[2], core, :, pl.ds(start, width)]

    sends, keeps = [], []

    def exchange(g, j):
        _, _, r = ORDERS[g]
        width = groups[g][1]
        for dr in range(RING):
            for dc in range(CORES):
                to, c = (me[r] + dr) % RING, (core + dc) % CORES
                src = out.at[g, j, to * CORES + c, :, :, :, pl.ds(0, width)]
                if dr == 0 and dc == 0:
                    copy = pltpu.make_async_copy(src, place_in(rx_ref, g, j), self_sem.at[g, j])
                    keeps.append(copy)
                else:
                    n = dr * CORES + dc
                    copy = pltpu.make_async_remote_copy(
                        src_ref=src, dst_ref=place_in(rx_ref, g, j),
                        send_sem=rsend.at[g, j, n], recv_sem=rrecv.at[g, j, n],
                        device_id=shifted(r, dr, c), device_id_type=pl.DeviceIdType.MESH)
                    sends.append(copy)
                copy.start()

    for g in everyone:
        choose(g, 0)
        exchange(g, 0)
    for i in (3, 1):
        for g in everyone:
            second_on(g, i)
    for g in everyone:
        second_on(g, 2)
    for j in (3, 1):
        for g in everyone:
            choose(g, j)
            exchange(g, j)
    for g in everyone:
        for i in range(RING):
            hops[g, 6 + 4 * i].wait_recv()
            hops[g, 7 + 4 * i].wait_recv()
        choose(g, 2)
        exchange(g, 2)

    for copy in sends:
        copy.wait_recv()
    for copy in keeps:
        copy.wait()
    for copy in hops.values():
        copy.wait_send()
    for copy in sends:
        copy.wait_send()


def dispatch(x, ids, cap):
    t, hd = x.shape
    groups = column_groups(hd)
    wide = max(w for _, w in groups)
    tail = jnp.full((IDROWS, hd), -1.0, bf16)
    for start, _ in groups:
        tail = lax.dynamic_update_slice(tail, ids.T.astype(bf16), (0, start))
    block = jnp.concatenate([x, tail], axis=0)
    n = len(groups)
    peers = RING * CORES
    return pl.pallas_call(
        functools.partial(dispatch_kernel, t, cap, groups),
        out_shape=jax.ShapeDtypeStruct((PARTS, RING, RING, RING, CORES, cap // PARTS, hd), bf16),
        in_specs=[pl.BlockSpec(memory_space=pl.ANY)],
        out_specs=pl.BlockSpec(memory_space=pl.ANY),
        scratch_shapes=[
            pltpu.VMEM((n, RING, RING, t + IDROWS, wide), bf16),
            pltpu.VMEM((n, RING, peers, PARTS, RING, cap // PARTS, wide), bf16),
            pltpu.VMEM((t, t), bf16),
            pltpu.VMEM((peers * cap, t), bf16),
            pltpu.SemaphoreType.DMA((n,)),
            pltpu.SemaphoreType.DMA((n, 4 + 4 * RING)),
            pltpu.SemaphoreType.DMA((n, 4 + 4 * RING)),
            pltpu.SemaphoreType.DMA((n, RING, peers)),
            pltpu.SemaphoreType.DMA((n, RING, peers)),
            pltpu.SemaphoreType.DMA((n, RING)),
        ],
        compiler_params=pltpu.CompilerParams(collective_id=0, has_side_effects=True, vmem_limit_bytes=60 * 2 ** 20),
        name="dispatch",
    )(block)


def solution(mesh):
    nx = mesh.shape["ex"]
    nd = mesh.shape["ey"] * nx
    axes = ("ey", "ex")
    tok = P(("dp", "ey", "ex"), None)
    wsp = P(("ey", "ex"), None, None)

    def top8(v):
        return lax.reduce_precision(jnp.minimum(v, float(jnp.finfo(bf16).max)), 8, 7)

    def split3(v):
        a = top8(v)
        b = top8(v - a)
        c = top8(v - a - b)
        return a.astype(bf16), b.astype(bf16), c.astype(bf16)

    def local(x, ids, gates, w1, w3, w2):
        t, hd = x.shape
        top = ids.shape[1]
        cap = min(t, CAPF * t * top // nd)
        half = cap // PARTS
        rx = dispatch(x, ids, cap)

        match = ids[:, :, None] == jnp.arange(nd)[None, None, :]
        hit = jnp.any(match, axis=1)
        gate = jnp.sum(jnp.where(match, gates[:, :, None], 0.0), axis=1)
        lower = (jnp.arange(t)[:, None] >= jnp.arange(t)[None, :]).astype(bf16)
        rank = jnp.dot(lower, hit.astype(bf16), preferred_element_type=f32).astype(jnp.int32) - 1
        slot = jnp.where(hit & (rank < cap), rank, cap)
        grow = (jnp.arange(nd)[:, None] == (jnp.arange(nd * half) // half)[None, :]).astype(bf16)
        wide = lambda v: jnp.dot(v, grow, preferred_element_type=f32)
        slots = wide(slot.astype(bf16))
        g = sum(wide(part) for part in split3(gate))

        moe = x.astype(f32)
        for h in range(PARTS):
            r = rx[h].reshape(nd * half, hd)
            a1 = jnp.dot(r, w1[0], preferred_element_type=f32)
            a3 = jnp.dot(r, w3[0], preferred_element_type=f32)
            hh = (jax.nn.silu(a1) * a3).astype(bf16)
            o = jnp.dot(hh, w2[0], preferred_element_type=f32)
            peak = jnp.maximum(jnp.max(jnp.abs(o), axis=1), 1e-34)
            o = (o * (FULL / peak)[:, None]).astype(f16)
            back = lax.all_to_all(o.reshape(nd, half, hd), axes, 0, 0, tiled=True).reshape(nd * half, hd)
            peak = lax.all_to_all(peak.reshape(nd, half), axes, 0, 0, tiled=True).reshape(1, nd * half)
            mine = slots == (jnp.arange(nd * half) % half + h * half).astype(f32)[None, :]
            wt = jnp.concatenate(split3(jnp.where(mine, g * (peak * (1.0 / FULL)), 0.0)), axis=0)
            wt = lax.optimization_barrier(wt)
            back = back.astype(f32)
            hi = top8(back)
            hi, lo = hi.astype(bf16), (back - hi).astype(bf16)
            acc = jnp.dot(wt, hi, preferred_element_type=f32) + jnp.dot(wt, lo, preferred_element_type=f32)
            moe = moe + (acc[:t] + acc[t:2 * t] + acc[2 * t:])
        return moe.astype(bf16)

    return jax.shard_map(local, mesh=mesh, in_specs=(tok, tok, tok, wsp, wsp, wsp),
                         out_specs=tok, check_vma=False)
```

time: 647 us -> 529 us (0.82)
  the two profiles are of different devices: /device:TPU:37 before, /device:TPU:29 now
where the time goes in v2:
time: 529 us; the launch traced here: 520 us
  waiting for transfers between devices  180 us (34%)
  Pallas kernels  133 us (25%)
  matrix products  115 us (22%)
  starting transfers between devices  45.8 us (9%)
  other arithmetic  31.4 us (6%)
  local copies, waits for them, and re-layouts  14.8 us (3%)
    all_to_all x2, waiting for transfers between devices, local(): lax.all_to_all(o.reshape(nd, half, hd), axes, 0, 0, tiled=True)  180 us
    pallas_call x1, Pallas kernels, dispatch(): pl.pallas_call(functools.partial(dispatch_kernel, t, cap, groups), out_sh...  133 us
    dot_general x2, matrix products, local(): o = jnp.dot(hh, w2[0], preferred_element_type=f32)  45.2 us
    all_to_all x2, starting transfers between devices, local(): lax.all_to_all(o.reshape(nd, half, hd), axes, 0, 0, tiled=True)  26.7 us
    dot_general x2, matrix products, local(): jnp.dot(wt, hi, preferred_element_type=f32)  21.3 us
    dot_general x2, matrix products, local(): jnp.dot(wt, lo, preferred_element_type=f32)  20.5 us
    dot_general x2, matrix products, local(): a1 = jnp.dot(r, w1[0], preferred_element_type=f32)  20.3 us
    all_to_all x2, starting transfers between devices, local(): lax.all_to_all(peak.reshape(nd, half), axes, 0, 0, tiled=True)  19.1 us
  transfers between devices with their start and end apart: 4, of which 2 were waited for; matrix products, arithmetic and copies ran while one was open for 17% of the time, Pallas kernels for 0%

profile of v2, /device:TPU:29, one launch (start us, length us, event | category | flops | bytes accessed | tf_op | source)
XLA Modules:
  0.0 520.0 jit_solution(14563970664727243424)
XLA Ops:
  0.0 0.8 convert_bitcast_fusion
  0.9 0.8 constant_dynamic-update-slice_fusion.1
  1.7 0.7 constant_dynamic-update-slice_fusion
  2.4 2.3 pad_maximum_fusion.2.x_ref
  4.7 133.0 %dispatch.1 = bf16[2,4,4,4,2,16,2048]{6,5,4,3,2,1,0:T(8,128)(2,1)} custom-call(bf16[264,2048]{1,0:T(8,128)(2,1)} %pad_maximum_fusion.2.x_ref), custom_call_target="tpu_custom_call" | custom-call | tf_op jit(solution)/shard_map/dispatch/pallas_call | solution.py:215
  137.7 9.7 %fusion.86 = (bf16[1,4,4,4,2,16,2048]{6,5,4,3,2,1,0:T(8,128)(2,1)}, bf16[1,4,4,4,2,16,2048]{6,5,4,3,2,1,0:T(8,128)(2,1)S(1)}) fusion(bf16[2,4,4,4,2,16,2048]{6,5,4,3,2,1,0:T(8,128)(2,1)} %dispatch.1), kind=kLoop, calls=%fused_computation.123 | loop fusion | bytes 33554432 | tf_op jit(solution)/shard_map/slice | solution.py:273
  147.4 3.2 copy-done.2
  150.7 8.6 %fusion.32 = f32[2048,768]{1,0:T(8,128)} fusion(bf16[2048,2048]{1,0:T(8,128)(2,1)S(1)} %bitcast.54, bf16[1,2048,768]{2,1,0:T(8,128)(2,1)S(1)} %copy-done.8), kind=kOutput, calls=%fused_computation.34 | convolution fusion | flops 6442450944 | bytes 17825792 | tf_op jit(solution)/shard_map/dot_general | solution.py:274
  159.2 22.6 %abs_reduce_fusion = (f32[2048]{0:T(1024)S(1)}, f32[2048,2048]{1,0:T(8,128)}) fusion(bf16[1,768,2048]{2,1,0:T(8,128)(2,1)S(1)} %copy-done, f32[2048,768]{1,0:T(8,128)} %fusion.32, bf16[2048,2048]{1,0:T(8,128)(2,1)} %bitcast.55, bf16[1,2048,768]{2,1,0:T(8,128)(2,1)} %param.10), kind=kOutput, calls=%fused_computation.11 | convolution fusion | flops 12902725632 | bytes 37756928 | tf_op jit(solution)/shard_map/dot_general | solution.py:277
  181.9 0.7 max.39
  182.6 9.3 %all-to-all-start.2 = ((f32[128,1,16]{2,1,0:T(1,128)}), f32[128,1,16]{2,1,0:T(1,128)S(1)}, u32[]{:S(2)}, u32[]{:S(2)}) async-start(f32[128,1,16]{2,1,0:T(1,128)} %bitcast.10), calls=%async_computation.2 | async-start | bytes 131072 | tf_op jit(solution)/shard_map/all_to_all | solution.py:281
  191.9 11.7 %fusion.34 = f32[2048,768]{1,0:T(8,128)} fusion(bf16[2048,2048]{1,0:T(8,128)(2,1)} %bitcast.52, bf16[1,2048,768]{2,1,0:T(8,128)(2,1)} %param.9), kind=kOutput, calls=%fused_computation.36 | convolution fusion | flops 6442450944 | bytes 17825792 | tf_op jit(solution)/shard_map/dot_general | solution.py:274
  203.6 22.6 %abs_reduce_fusion.1 = (f32[2048]{0:T(1024)S(1)}, f32[2048,2048]{1,0:T(8,128)}) fusion(bf16[1,768,2048]{2,1,0:T(8,128)(2,1)S(1)} %copy-done, f32[2048,768]{1,0:T(8,128)} %fusion.34, bf16[2048,2048]{1,0:T(8,128)(2,1)} %bitcast.53, bf16[1,2048,768]{2,1,0:T(8,128)(2,1)} %param.10), kind=kOutput, calls=%fused_computation.13 | convolution fusion | flops 12902725632 | bytes 37756928 | tf_op jit(solution)/shard_map/dot_general | solution.py:277
  226.2 0.7 max.37
  227.0 9.8 %all-to-all-start = ((f32[128,1,16]{2,1,0:T(1,128)}), f32[128,1,16]{2,1,0:T(1,128)S(1)}, u32[]{:S(2)}, u32[]{:S(2)}) async-start(f32[128,1,16]{2,1,0:T(1,128)} %bitcast.5), calls=%async_computation | async-start | bytes 131072 | tf_op jit(solution)/shard_map/all_to_all | solution.py:281
  236.7 9.4 %multiply_convert_fusion.1 = f16[2048,2048]{1,0:T(8,128)(2,1)} fusion(f32[2048,2048]{1,0:T(8,128)} %get-tuple-element.22, f32[2048]{0:T(1024)S(1)} %get-tuple-element.17), kind=kLoop, calls=%fused_computation.12 | loop fusion | flops 8388608 | bytes 25174016 | tf_op jit(solution)/shard_map/convert_element_type | solution.py:279
  246.1 10.2 %all-to-all-start.1 = ((f16[128,16,2048]{2,1,0:T(8,128)(2,1)}), f16[128,16,2048]{2,1,0:T(8,128)(2,1)}, u32[]{:S(2)}, u32[]{:S(2)}) async-start(f16[128,16,2048]{2,1,0:T(8,128)(2,1)} %bitcast.51), calls=%async_computation.1 | async-start | bytes 16777216 | tf_op jit(solution)/shard_map/all_to_all | solution.py:280
  256.3 9.4 %multiply_convert_fusion = f16[2048,2048]{1,0:T(8,128)(2,1)} fusion(f32[2048,2048]{1,0:T(8,128)} %get-tuple-element.24, f32[2048]{0:T(1024)S(1)} %get-tuple-element.19), kind=kLoop, calls=%fused_computation.10 | loop fusion | flops 8388608 | bytes 25174016 | tf_op jit(solution)/shard_map/convert_element_type | solution.py:279
  265.7 98.8 %all-to-all-done.1 = f16[128,16,2048]{2,1,0:T(8,128)(2,1)} async-done(((f16[128,16,2048]{2,1,0:T(8,128)(2,1)}), f16[128,16,2048]{2,1,0:T(8,128)(2,1)}, u32[]{:S(2)}, u32[]{:S(2)}) %all-to-all-start.1) | async-done | bytes 8388640 | tf_op jit(solution)/shard_map/all_to_all | solution.py:280
  364.5 16.5 %all-to-all-start.3 = ((f16[128,16,2048]{2,1,0:T(8,128)(2,1)}), f16[128,16,2048]{2,1,0:T(8,128)(2,1)}, u32[]{:S(2)}, u32[]{:S(2)}) async-start(f16[128,16,2048]{2,1,0:T(8,128)(2,1)} %bitcast.50), calls=%async_computation.3 | async-start | bytes 16777216 | tf_op jit(solution)/shard_map/all_to_all | solution.py:280
  381.8 1.3 select_reduce_fusion
  383.0 2.0 fusion.49
  385.5 1.8 convolution_add_fusion.1
  387.8 3.2 fusion.46
  391.0 1.2 fusion.41
  392.2 1.9 pad_maximum_fusion.1
  394.5 9.2 %fusion.10 = f32[768,2048]{1,0:T(8,128)S(1)} fusion(bf16[768,2048]{1,0:T(8,128)(2,1)S(1)} %pad_maximum_fusion, f16[2048,2048]{1,0:T(8,128)(2,1)} %bitcast.8), kind=kOutput, calls=%fused_computation.16 | convolution fusion | flops 6463422464 | bytes 17825792 | tf_op jit(solution)/shard_map/dot_general | solution.py:288
  403.8 11.0 %fusion.20 = f32[768,2048]{1,0:T(8,128)} fusion(f32[768,2048]{1,0:T(8,128)S(1)} %fusion.10, bf16[768,2048]{1,0:T(8,128)(2,1)S(1)} %pad_maximum_fusion, f16[2048,2048]{1,0:T(8,128)(2,1)} %bitcast.8), kind=kOutput, calls=%fused_computation.26 | convolution fusion | flops 6460801024 | bytes 24117248 | tf_op jit(solution)/shard_map/dot_general | solution.py:288
  414.8 80.7 %all-to-all-done.3 = f16[128,16,2048]{2,1,0:T(8,128)(2,1)} async-done(((f16[128,16,2048]{2,1,0:T(8,128)(2,1)}), f16[128,16,2048]{2,1,0:T(8,128)(2,1)}, u32[]{:S(2)}, u32[]{:S(2)}) %all-to-all-start.3) | async-done | bytes 8388640 | tf_op jit(solution)/shard_map/all_to_all | solution.py:280
  495.6 11.3 %fusion.6 = f32[768,2048]{1,0:T(8,128)} fusion(bf16[768,2048]{1,0:T(8,128)(2,1)S(1)} %copy-done.4, f16[2048,2048]{1,0:T(8,128)(2,1)} %bitcast.13), kind=kOutput, calls=%fused_computation.14 | convolution fusion | flops 6463422464 | bytes 17825792 | tf_op jit(solution)/shard_map/dot_general | solution.py:288
  506.8 10.3 %fusion.23 = f32[768,2048]{1,0:T(8,128)S(1)} fusion(f32[768,2048]{1,0:T(8,128)} %fusion.6, bf16[768,2048]{1,0:T(8,128)(2,1)S(1)} %copy-done.5, f16[2048,2048]{1,0:T(8,128)(2,1)} %bitcast.13), kind=kOutput, calls=%fused_computation.27 | convolution fusion | flops 6460801024 | bytes 24117248 | tf_op jit(solution)/shard_map/dot_general | solution.py:288
  517.1 2.4 fusion.39
  (39 shorter events, 2.2 us)
Async XLA Ops:
  0.0 159.2 %copy-start = (bf16[1,768,2048]{2,1,0:T(8,128)(2,1)S(1)}, bf16[1,768,2048]{2,1,0:T(8,128)(2,1)}, u32[]{:S(2)}) copy-start(bf16[1,768,2048]{2,1,0:T(8,128)(2,1)} %param.11) | copy-start | bytes 9437188
  137.7 13.0 %copy-start.8 = (bf16[1,2048,768]{2,1,0:T(8,128)(2,1)S(1)}, bf16[1,2048,768]{2,1,0:T(8,128)(2,1)}, u32[]{:S(2)}) copy-start(bf16[1,2048,768]{2,1,0:T(8,128)(2,1)} %param.9) | copy-start | bytes 9437188
  147.4 3.2 copy-start.2
  182.6 44.4 %all-to-all-start.2 = ((f32[128,1,16]{2,1,0:T(1,128)}), f32[128,1,16]{2,1,0:T(1,128)S(1)}, u32[]{:S(2)}, u32[]{:S(2)}) async-start(f32[128,1,16]{2,1,0:T(1,128)} %bitcast.10), calls=%async_computation.2 | async-start | bytes 131072 | tf_op jit(solution)/shard_map/all_to_all | solution.py:281
  227.0 19.2 %all-to-all-start = ((f32[128,1,16]{2,1,0:T(1,128)}), f32[128,1,16]{2,1,0:T(1,128)S(1)}, u32[]{:S(2)}, u32[]{:S(2)}) async-start(f32[128,1,16]{2,1,0:T(1,128)} %bitcast.5), calls=%async_computation | async-start | bytes 131072 | tf_op jit(solution)/shard_map/all_to_all | solution.py:281
  246.1 118.4 %all-to-all-start.1 = ((f16[128,16,2048]{2,1,0:T(8,128)(2,1)}), f16[128,16,2048]{2,1,0:T(8,128)(2,1)}, u32[]{:S(2)}, u32[]{:S(2)}) async-start(f16[128,16,2048]{2,1,0:T(8,128)(2,1)} %bitcast.51), calls=%async_computation.1 | async-start | bytes 16777216 | tf_op jit(solution)/shard_map/all_to_all | solution.py:280
  364.5 16.5 %copy-start.6 = (s32[256,8]{0,1:T(8,128)S(1)}, s32[256,8]{0,1:T(8,128)}, u32[]{:S(2)}) copy-start(s32[256,8]{0,1:T(8,128)} %param.7) | copy-start | bytes 24580
  364.5 16.6 %copy-start.7 = (f32[256,8]{0,1:T(8,128)S(1)}, f32[256,8]{0,1:T(8,128)}, u32[]{:S(2)}) copy-start(f32[256,8]{0,1:T(8,128)} %param.8) | copy-start | bytes 24580
  364.5 131.0 %all-to-all-start.3 = ((f16[128,16,2048]{2,1,0:T(8,128)(2,1)}), f16[128,16,2048]{2,1,0:T(8,128)(2,1)}, u32[]{:S(2)}, u32[]{:S(2)}) async-start(f16[128,16,2048]{2,1,0:T(8,128)(2,1)} %bitcast.50), calls=%async_computation.3 | async-start | bytes 16777216 | tf_op jit(solution)/shard_map/all_to_all | solution.py:280
  403.8 91.8 %copy-start.4 = (bf16[768,2048]{1,0:T(8,128)(2,1)S(1)}, bf16[768,2048]{1,0:T(8,128)(2,1)}, u32[]{:S(2)}) copy-start(bf16[768,2048]{1,0:T(8,128)(2,1)} %pad_maximum_fusion.1) | copy-start | bytes 9437188
  495.6 11.3 %copy-start.5 = (bf16[768,2048]{1,0:T(8,128)(2,1)S(1)}, bf16[768,2048]{1,0:T(8,128)(2,1)}, u32[]{:S(2)}) copy-start(bf16[768,2048]{1,0:T(8,128)(2,1)} %pad_maximum_fusion.1) | copy-start | bytes 9437188
  495.6 21.5 %slice-start = ((s8[6291456]{0:T(1024)(128)(4,1)}), s8[4194304]{0:T(1024)(128)(4,1)S(1)}, s32[]{:S(2)}) async-start(s8[6291456]{0:T(1024)(128)(4,1)} %bitcast.56), calls=%async_computation.4 | async-start | bytes 8388608
  506.8 10.3 %slice-start.1 = ((s8[6291456]{0:T(1024)(128)(4,1)}), s8[2097152]{0:T(1024)(128)(4,1)S(1)}, s32[]{:S(2)}) async-start(s8[6291456]{0:T(1024)(128)(4,1)} %bitcast.56), calls=%async_computation.5 | async-start | bytes 4194304
  506.8 10.3 %copy-start.3 = (bf16[256,2048]{1,0:T(8,128)(2,1)S(1)}, bf16[256,2048]{1,0:T(8,128)(2,1)}, u32[]{:S(2)}) copy-start(bf16[256,2048]{1,0:T(8,128)(2,1)} %param.6) | copy-start | bytes 3145732
  506.8 12.8 %copy-start.1 = (bf16[1,768,2048]{2,1,0:T(8,128)(2,1)S(1)}, bf16[1,768,2048]{2,1,0:T(8,128)(2,1)}, u32[]{:S(2)}) copy-start(bf16[1,768,2048]{2,1,0:T(8,128)(2,1)} %param.11) | copy-start | bytes 9437188

commit v3 on v2

--- a/solution.py
+++ b/solution.py
@@ -8,20 +8,25 @@
 from jax.sharding import PartitionSpec as P
 
 CAPF = 2
-FULL = 16384.0
+FULL = 32000.0
 RING = 4
 CORES = 2
-PARTS = 2
 IDROWS = 8
 ORDERS = ((0, 1, 2), (2, 0, 1), (1, 2, 0))
-bf16, f16, f32 = jnp.bfloat16, jnp.float16, jnp.float32
-
-
-def column_groups(hd):
-    tiles = hd // 128
+LINE = RING * CORES
+STRIDES = (RING * RING * CORES, RING * CORES, CORES)
+RETURNS = ((2, 1, 0), (1, 0, 2), (0, 2, 1))
+TILE = 256
+SLOTS = 4
+MESH = pl.DeviceIdType.MESH
+bf16, i16, f32 = jnp.bfloat16, jnp.int16, jnp.float32
+
+
+def column_groups(hd, tile):
+    tiles = hd // tile
     first = -(-tiles // 3)
     second = -(-(tiles - first) // 2)
-    widths = [first * 128, second * 128, (tiles - first - second) * 128]
+    widths = [first * tile, second * tile, (tiles - first - second) * tile]
     starts = [0, widths[0], widths[0] + widths[1]]
     return list(zip(starts, widths))
 
@@ -30,7 +35,6 @@
     ey, ex, dp = lax.axis_index("ey"), lax.axis_index("ex"), lax.axis_index("dp")
     me = [ey // RING, ey % RING, ex // CORES]
     core = ex % CORES
-    half = cap // PARTS
     rows = t + IDROWS
     split = (rows // 2 + 7) // 8 * 8
 
@@ -52,7 +56,7 @@
     peers = [(axis, by, dc) for axis in range(3) for by in range(1, RING) for dc in range(CORES)] + [(0, 0, 1)]
     for axis, by, dc in peers:
         pl.semaphore_signal(barrier, inc=1, device_id=shifted(axis, by, (core + dc) % CORES),
-                            device_id_type=pl.DeviceIdType.MESH)
+                            device_id_type=MESH)
     row = lax.broadcasted_iota(jnp.int32, (t, t), 0)
     col = lax.broadcasted_iota(jnp.int32, (t, t), 1)
     upper[...] = jnp.where(row <= col, 1.0, 0.0).astype(bf16)
@@ -67,7 +71,7 @@
             src_ref=got.at[g, block[0], block[1], at, pl.ds(0, width)],
             dst_ref=got.at[g, to[0], to[1], at, pl.ds(0, width)],
             send_sem=gsend.at[g, index], recv_sem=grecv.at[g, index],
-            device_id=shifted(axis, by), device_id_type=pl.DeviceIdType.MESH)
+            device_id=shifted(axis, by), device_id_type=MESH)
         copy.start()
         hops[g, index] = copy
 
@@ -134,9 +138,7 @@
                 at = pl.ds(pl.multiple_of(n * 128, 128), 128)
                 val = jnp.dot(pick[...], got[g, i, j, pl.ds(0, t), at], preferred_element_type=f32).astype(bf16)
                 for k in range(RING * CORES):
-                    for h in range(PARTS):
-                        begin = k * cap + h * half
-                        out[g, j, k, h, place, :, at] = val[begin:begin + half]
+                    out[g, j, k, place, :, at] = val[k * cap:(k + 1) * cap]
                 return 0
 
             return lax.fori_loop(0, width // 128, tile, 0)
@@ -150,7 +152,7 @@
         at[p] = slice(None)
         at[q] = (me[q] + j) % RING
         at[r] = me[r]
-        return ref.at[:, at[0], at[1], at[2], core, :, pl.ds(start, width)]
+        return ref.at[at[0], at[1], at[2], core, :, pl.ds(start, width)]
 
     sends, keeps = [], []
 
@@ -160,7 +162,7 @@
         for dr in range(RING):
             for dc in range(CORES):
                 to, c = (me[r] + dr) % RING, (core + dc) % CORES
-                src = out.at[g, j, to * CORES + c, :, :, :, pl.ds(0, width)]
+                src = out.at[g, j, to * CORES + c, :, :, pl.ds(0, width)]
                 if dr == 0 and dc == 0:
                     copy = pltpu.make_async_copy(src, place_in(rx_ref, g, j), self_sem.at[g, j])
                     keeps.append(copy)
@@ -169,7 +171,7 @@
                     copy = pltpu.make_async_remote_copy(
                         src_ref=src, dst_ref=place_in(rx_ref, g, j),
                         send_sem=rsend.at[g, j, n], recv_sem=rrecv.at[g, j, n],
-                        device_id=shifted(r, dr, c), device_id_type=pl.DeviceIdType.MESH)
+                        device_id=shifted(r, dr, c), device_id_type=MESH)
                     sends.append(copy)
                 copy.start()
 
@@ -204,7 +206,7 @@
 
 def dispatch(x, ids, cap):
     t, hd = x.shape
-    groups = column_groups(hd)
+    groups = column_groups(hd, 128)
     wide = max(w for _, w in groups)
     tail = jnp.full((IDROWS, hd), -1.0, bf16)
     for start, _ in groups:
@@ -214,12 +216,12 @@
     peers = RING * CORES
     return pl.pallas_call(
         functools.partial(dispatch_kernel, t, cap, groups),
-        out_shape=jax.ShapeDtypeStruct((PARTS, RING, RING, RING, CORES, cap // PARTS, hd), bf16),
+        out_shape=jax.ShapeDtypeStruct((RING, RING, RING, CORES, cap, hd), bf16),
         in_specs=[pl.BlockSpec(memory_space=pl.ANY)],
         out_specs=pl.BlockSpec(memory_space=pl.ANY),
         scratch_shapes=[
             pltpu.VMEM((n, RING, RING, t + IDROWS, wide), bf16),
-            pltpu.VMEM((n, RING, peers, PARTS, RING, cap // PARTS, wide), bf16),
+            pltpu.VMEM((n, RING, peers, RING, cap, wide), bf16),
             pltpu.VMEM((t, t), bf16),
             pltpu.VMEM((peers * cap, t), bf16),
             pltpu.SemaphoreType.DMA((n,)),
@@ -234,60 +236,379 @@
     )(block)
 
 
+def experts_kernel(t, cap, groups, info_ref, x_ref, rx_ref, w1_ref, w3_ref, w2_ref, y_ref, r2,
+                   w1, w3, w2, xb, hh, res, ob, so, r1, s1, s2, acc, planes, info, db, wt, upper,
+                   wsem, xsem, isend, irecv, p1s, p1r, q1s, q1r, p2s, p2r, q2s, q2r, p3s, p3r, dsem):
+    ey, ex, dp = lax.axis_index("ey"), lax.axis_index("ex"), lax.axis_index("dp")
+    me = [ey // RING, ey % RING, ex // CORES]
+    core = ex % CORES
+    rows = LINE * cap
+    hd, ff = w1.shape
+    everyone = range(len(groups))
+    col0 = [start for start, _ in groups]
+    width = [w for _, w in groups]
+    own = [me[RETURNS[g][0]] * CORES + core for g in everyone]
+
+    def shifted(axis, by, c=None):
+        coords = list(me)
+        coords[axis] = (coords[axis] + by) % RING
+        return (dp, coords[0] * RING + coords[1], coords[2] * CORES + (core if c is None else c))
+
+    def remote(src, dst, send, recv, to):
+        return pltpu.make_async_remote_copy(src_ref=src, dst_ref=dst, send_sem=send, recv_sem=recv,
+                                            device_id=to, device_id_type=MESH)
+
+    loads = [pltpu.make_async_copy(a, b, wsem.at[n])
+             for n, (a, b) in enumerate(((w1_ref, w1), (w3_ref, w3), (w2_ref, w2)))]
+    for load in loads:
+        load.start()
+
+    def homes(step):
+        return (step + step // RING) % RING, step % RING
+
+    def tile_load(step):
+        dz, dy = homes(step)
+        return pltpu.make_async_copy(rx_ref.at[(me[0] + dz) % RING, (me[1] + dy) % RING], xb.at[step % 2], xsem.at[step % 2])
+
+    tile_load(0).start()
+
+    barrier = pltpu.get_barrier_semaphore()
+    peers = [(axis, by, dc) for axis in range(3) for by in range(1, RING) for dc in range(CORES)] + [(0, 0, 1)]
+    for axis, by, dc in peers:
+        pl.semaphore_signal(barrier, inc=1, device_id=shifted(axis, by, (core + dc) % CORES), device_id_type=MESH)
+    row = lax.broadcasted_iota(jnp.int32, (t, t), 0)
+    col = lax.broadcasted_iota(jnp.int32, (t, t), 1)
+    upper[...] = jnp.where(row <= col, 1.0, 0.0).astype(bf16)
+    for axis in range(3):
+        info[axis, me[axis]] = info_ref[...]
+    pl.semaphore_wait(barrier, len(peers))
+
+    told = []
+    for axis in range(3):
+        for by in range(1, RING):
+            told.append(remote(info_ref, info.at[axis, me[axis]], isend.at[axis, by], irecv.at[axis, by], shifted(axis, by)))
+            told[-1].start()
+
+    for load in loads:
+        load.wait()
+
+    def first(step):
+        dz, dy = homes(step)
+        zh, yh = (me[0] + dz) % RING, (me[1] + dy) % RING
+        slot = step % SLOTS
+        found = []
+        for n in range(1, LINE):
+            d, dc = n // CORES, n % CORES
+            c = (core + dc) % CORES
+            found.append((None, remote(
+                ob.at[slot, (me[2] + d) % RING, c, :, pl.ds(col0[0], width[0])],
+                r1.at[0, own[0], zh, yh, :, pl.ds(0, width[0])],
+                p1s.at[slot, n], p1r.at[0, n], shifted(2, d, c))))
+        for g, axis, d, lead in ((1, 1, dy, zh), (2, 0, dz, yh)):
+            for dc in range(CORES):
+                c = (core + dc) % CORES
+                found.append((None if dc else d != 0, remote(
+                    ob.at[slot, :, c, :, pl.ds(col0[g], width[g])],
+                    r1.at[g, own[g], lead, :, :, pl.ds(0, width[g])],
+                    p1s.at[slot, LINE + 2 * (g - 1) + dc], p1r.at[g, d * CORES + dc], shifted(axis, d, c))))
+        return found
+
+    def each(found, act):
+        for whether, copy in found:
+            if whether is None:
+                act(copy)
+            else:
+                @pl.when(whether)
+                def _():
+                    act(copy)
+
+    eye = lax.broadcasted_iota(jnp.int32, (cap, 128), 0) == lax.broadcasted_iota(jnp.int32, (cap, 128), 1)
+
+    def tile(step, _):
+        dz, dy = homes(step)
+        zh, yh = (me[0] + dz) % RING, (me[1] + dy) % RING
+        slot = step % SLOTS
+
+        @pl.when(step + 1 < RING * RING)
+        def _():
+            tile_load(step + 1).start()
+
+        tile_load(step).wait()
+
+        def up(n, _):
+            at = pl.ds(pl.multiple_of(n * TILE, TILE), TILE)
+            xt = xb[step % 2].reshape(rows, hd)
+            a1 = jnp.dot(xt, w1[:, at], preferred_element_type=f32)
+            a3 = jnp.dot(xt, w3[:, at], preferred_element_type=f32)
+            hh[:, at] = (a1 * (1.0 / (1.0 + jnp.exp(-a1))) * a3).astype(bf16)
+            return 0
+
+        lax.fori_loop(0, ff // TILE, up, 0)
+
+        def down(n, peak):
+            at = pl.ds(pl.multiple_of(n * TILE, TILE), TILE)
+            o = jnp.dot(hh[...], w2[:, at], preferred_element_type=f32)
+            res[:, at] = o
+            return jnp.maximum(peak, jnp.max(jnp.abs(o), axis=1, keepdims=True))
+
+        peak = lax.fori_loop(0, hd // TILE, down, jnp.full((rows, 1), 1e-30, f32))
+        for k in range(LINE):
+            part = jnp.where(eye, peak[k * cap:(k + 1) * cap], 0.0)
+            so[zh, yh, k // CORES, k % CORES] = jnp.sum(part, axis=0, keepdims=True) * (1.0 / FULL)
+
+        @pl.when(step >= SLOTS)
+        def _():
+            each(first(step - SLOTS), lambda copy: copy.wait_send())
+
+        factor = FULL / peak
+
+        def code(n, _):
+            at = pl.ds(pl.multiple_of(n * TILE, TILE), TILE)
+            v = jnp.round(res[:, at] * factor).astype(jnp.int32).astype(i16)
+            ob[slot, :, :, :, at] = v.reshape(RING, CORES, cap, TILE)
+            return 0
+
+        lax.fori_loop(0, hd // TILE, code, 0)
+        each(first(step), lambda copy: copy.start())
+
+        r1[0, own[0], zh, yh, :, pl.ds(0, width[0])] = ob[slot, me[2], core, :, pl.ds(col0[0], width[0])]
+        for g, d, lead in ((1, dy, zh), (2, dz, yh)):
+            @pl.when(d == 0)
+            def _():
+                for xh in range(RING):
+                    r1[g, own[g], lead, xh, :, pl.ds(0, width[g])] = ob[slot, xh, core, :, pl.ds(col0[g], width[g])]
+        return 0
+
+    lax.fori_loop(0, RING * RING, tile, 0)
+
+    def scales(g, coord, c):
+        return (so.at[:, :, coord, c], so.at[:, coord, :, c], so.at[coord, :, :, c])[g]
+
+    hints = []
+    for g in everyone:
+        axis = RETURNS[g][0]
+        s1[g, own[g]] = (so[:, :, me[2], core], so[:, me[1], :, core], so[me[0], :, :, core])[g]
+        for n in range(1, LINE):
+            d, dc = n // CORES, n % CORES
+            c = (core + dc) % CORES
+            hints.append(remote(scales(g, (me[axis] + d) % RING, c), s1.at[g, own[g]],
+                                q1s.at[g, n], q1r.at[g, n], shifted(axis, d, c)))
+            hints[-1].start()
+
+    for g in everyone:
+        axis = RETURNS[g][0]
+        for n in range(1, LINE):
+            d, dc = n // CORES, n % CORES
+            src = (me[axis] - d) % RING * CORES + (core + dc) % CORES
+            ref = r1.at[g, src, :, :, :, pl.ds(0, width[g])]
+            pltpu.make_async_copy(ref, ref, p1r.at[g, n]).wait()
+    for copy in hints:
+        copy.wait_recv()
+
+    def lane(ref, g, h2, h3):
+        return (ref.at[0, :, h3, h2], ref.at[1, :, h2, h3], ref.at[2, :, h3, h2])[g]
+
+    moved = []
+    for g in everyone:
+        axis = RETURNS[g][1]
+        s2[g, me[axis]] = (s1[0, :, :, me[1]], s1[1, :, me[0]], s1[2, :, :, me[2]])[g]
+        for d in (1, 3, 2):
+            moved.append(remote(lane(s1, g, (me[axis] + d) % RING, slice(None)), s2.at[g, me[axis]],
+                                q2s.at[g, d], q2r.at[g, d], shifted(axis, d)))
+            moved[-1].start()
+
+    def second(g, k3, d):
+        _, axis, third = RETURNS[g]
+        h3 = (me[third] + k3) % RING
+        src = (r1.at[0, :, h3, (me[axis] + d) % RING, :, pl.ds(0, width[0])] if g == 0 else
+               r1.at[1, :, (me[axis] + d) % RING, h3, :, pl.ds(0, width[1])] if g == 1 else
+               r1.at[2, :, h3, (me[axis] + d) % RING, :, pl.ds(0, width[2])])
+        return remote(src, r2.at[g, h3, me[axis], :, :, pl.ds(0, width[g])],
+                      p2s.at[g, k3, d], p2r.at[g, k3, d], shifted(axis, d))
+
+    for k3 in (1, 2, 3, 0):
+        for d in (1, 3, 2):
+            for g in everyone:
+                second(g, k3, d).start()
+
+    for copy in told:
+        copy.wait_recv()
+    for copy in moved:
+        copy.wait_recv()
+
+    wanted = lax.broadcasted_iota(jnp.int32, (cap, t), 0).astype(f32)
+
+    def weights(g, h3, src):
+        first_axis, axis, third = RETURNS[g]
+        ids = info[third, h3, 0:8, :]
+        gates = info[third, h3, 8:16, :]
+        base = src * STRIDES[axis] + me[third] * STRIDES[third]
+        hits, gate = [], []
+        for k in range(LINE):
+            same = ids == (base + (k // CORES) * STRIDES[first_axis] + k % CORES).astype(f32)
+            hits.append(jnp.sum(jnp.where(same, 1.0, 0.0), axis=0, keepdims=True))
+            gate.append(jnp.sum(jnp.where(same, gates, 0.0), axis=0, keepdims=True))
+        hit = jnp.concatenate(hits, axis=0)
+        rank = jnp.dot(hit.astype(bf16), upper[...], preferred_element_type=f32)
+        slot = jnp.where((hit > 0.5) & (rank < cap + 0.5), rank - 1.0, -1.0)
+        for k in range(LINE):
+            scale = jnp.sum(jnp.where(eye, s2[g, src, k, h3], 0.0), axis=1, keepdims=True)
+            w = jnp.where(slot[k:k + 1, :] == wanted, gate[k], 0.0) * scale
+            a = w.astype(bf16)
+            w = w - a.astype(f32)
+            b = w.astype(bf16)
+            w = w - b.astype(f32)
+            at = pl.ds(k * cap, cap)
+            wt[at, pl.ds(0, t)] = a
+            wt[at, pl.ds(t, t)] = b
+            wt[at, pl.ds(2 * t, t)] = w.astype(bf16)
+
+    def line(index, _):
+        k3 = (index + 1) % RING
+
+        def plane(turn, _):
+            d = turn + turn // 2 - 2 * (turn // 3)
+
+            def fetch(g):
+                third = RETURNS[g][2]
+                src = (me[RETURNS[g][1]] - d) % RING
+                return pltpu.make_async_copy(r2.at[g, (me[third] + k3) % RING, src, :, :, pl.ds(0, width[g])],
+                                             db.at[g, :, :, pl.ds(0, width[g])], dsem.at[g])
+
+            for g in everyone:
+                _, axis, third = RETURNS[g]
+                h3 = (me[third] + k3) % RING
+
+                @pl.when(turn == 0)
+                def _():
+                    at = pl.ds(0, width[g])
+                    if g == 1:
+                        db[g, :, :, at] = r1[g, :, me[axis], h3, :, at]
+                    else:
+                        db[g, :, :, at] = r1[g, :, h3, me[axis], :, at]
+                    acc[g, index] = jnp.zeros(acc.shape[2:], f32)
+
+                @pl.when(turn > 0)
+                def _():
+                    second(g, k3, d).wait_recv()
+                    fetch(g).start()
+
+            for g in everyone:
+                _, axis, third = RETURNS[g]
+                weights(g, (me[third] + k3) % RING, (me[axis] - d) % RING)
+
+                @pl.when(turn > 0)
+                def _():
+                    fetch(g).wait()
+
+                def piece(n, _):
+                    at = pl.ds(pl.multiple_of(n * TILE, TILE), TILE)
+                    q = db[g, :, :, at].reshape(rows, TILE).astype(f32)
+                    high = q.astype(bf16)
+                    low = (q - high.astype(f32)).astype(bf16)
+                    dims = (((0,), (0,)), ((), ()))
+                    p = (lax.dot_general(wt[...], high, dims, preferred_element_type=f32)
+                         + lax.dot_general(wt[...], low, dims, preferred_element_type=f32))
+                    acc[g, index, :, at] += p[0:t] + p[t:2 * t] + p[2 * t:]
+                    return 0
+
+                lax.fori_loop(0, width[g] // TILE, piece, 0)
+            return 0
+
+        lax.fori_loop(0, RING, plane, 0)
+
+        @pl.when(index < RING - 1)
+        def _():
+            for g in everyone:
+                home(g, index).start()
+        return 0
+
+    def home(g, index):
+        at = pl.ds(0, width[g])
+        return remote(acc.at[g, index, :, at], planes.at[g, index, :, at],
+                      p3s.at[g, index], p3r.at[g, index], shifted(RETURNS[g][2], (index + 1) % RING))
+
+    lax.fori_loop(0, RING, line, 0)
+
+    for g in everyone:
+        for index in range(RING - 1):
+            home(g, index).wait_recv()
+        for n in range(width[g] // TILE):
+            at = pl.ds(n * TILE, TILE)
+            to = pl.ds(col0[g] + n * TILE, TILE)
+            total = acc[g, RING - 1, :, at] + planes[g, 0, :, at] + planes[g, 1, :, at] + planes[g, 2, :, at]
+            y_ref[:, to] = (x_ref[:, to].astype(f32) + total).astype(bf16)
+
+    for copy in told + hints + moved:
+        copy.wait_send()
+
+    def last(step, _):
+        each(first(step), lambda copy: copy.wait_send())
+        return 0
+
+    lax.fori_loop(RING * RING - SLOTS, RING * RING, last, 0)
+    for g in everyone:
+        for k3 in range(RING):
+            for d in (1, 3, 2):
+                second(g, k3, d).wait_send()
+        for index in range(RING - 1):
+            home(g, index).wait_send()
+
+
+def experts(x, ids, gates, rx, w1, w3, w2):
+    t, hd = x.shape
+    ff = w1.shape[1]
+    cap = rx.shape[4]
+    groups = column_groups(hd, TILE)
+    wide = max(w for _, w in groups)
+    n = len(groups)
+    info = jnp.concatenate([ids.T.astype(f32), gates.T], axis=0)
+    dma = pltpu.SemaphoreType.DMA
+    anywhere = pl.BlockSpec(memory_space=pl.ANY)
+    vmem = pl.BlockSpec(memory_space=pltpu.VMEM)
+    y, _ = pl.pallas_call(
+        functools.partial(experts_kernel, t, cap, groups),
+        out_shape=(jax.ShapeDtypeStruct((t, hd), bf16),
+                   jax.ShapeDtypeStruct((n, RING, RING, LINE, cap, wide), i16)),
+        in_specs=[vmem, vmem] + [anywhere] * 4,
+        out_specs=(vmem, anywhere),
+        scratch_shapes=[
+            pltpu.VMEM((hd, ff), bf16), pltpu.VMEM((hd, ff), bf16), pltpu.VMEM((ff, hd), bf16),
+            pltpu.VMEM((2, RING, CORES, cap, hd), bf16),
+            pltpu.VMEM((LINE * cap, ff), bf16),
+            pltpu.VMEM((LINE * cap, hd), f32),
+            pltpu.VMEM((SLOTS, RING, CORES, cap, hd), i16),
+            pltpu.VMEM((RING, RING, RING, CORES, 1, 128), f32),
+            pltpu.VMEM((n, LINE, RING, RING, cap, wide), i16),
+            pltpu.VMEM((n, LINE, RING, RING, 1, 128), f32),
+            pltpu.VMEM((n, RING, LINE, RING, 1, 128), f32),
+            pltpu.VMEM((n, RING, t, wide), f32),
+            pltpu.VMEM((n, RING - 1, t, wide), f32),
+            pltpu.VMEM((3, RING, 16, t), f32),
+            pltpu.VMEM((n, LINE, cap, wide), i16),
+            pltpu.VMEM((LINE * cap, 3 * t), bf16),
+            pltpu.VMEM((t, t), bf16),
+            dma((3,)), dma((2,)), dma((3, RING)), dma((3, RING)),
+            dma((SLOTS, LINE + 4)), dma((n, LINE)), dma((n, LINE)), dma((n, LINE)),
+            dma((n, RING, RING)), dma((n, RING, RING)), dma((n, RING)), dma((n, RING)),
+            dma((n, RING)), dma((n, RING)), dma((n,)),
+        ],
+        compiler_params=pltpu.CompilerParams(collective_id=1, has_side_effects=True, vmem_limit_bytes=67043328),
+        name="experts",
+    )(info, x, rx, w1, w3, w2)
+    return y
+
+
 def solution(mesh):
-    nx = mesh.shape["ex"]
-    nd = mesh.shape["ey"] * nx
-    axes = ("ey", "ex")
+    nd = mesh.shape["ey"] * mesh.shape["ex"]
     tok = P(("dp", "ey", "ex"), None)
     wsp = P(("ey", "ex"), None, None)
 
-    def top8(v):
-        return lax.reduce_precision(jnp.minimum(v, float(jnp.finfo(bf16).max)), 8, 7)
-
-    def split3(v):
-        a = top8(v)
-        b = top8(v - a)
-        c = top8(v - a - b)
-        return a.astype(bf16), b.astype(bf16), c.astype(bf16)
-
     def local(x, ids, gates, w1, w3, w2):
-        t, hd = x.shape
-        top = ids.shape[1]
-        cap = min(t, CAPF * t * top // nd)
-        half = cap // PARTS
+        t = x.shape[0]
+        cap = min(t, CAPF * t * ids.shape[1] // nd)
         rx = dispatch(x, ids, cap)
-
-        match = ids[:, :, None] == jnp.arange(nd)[None, None, :]
-        hit = jnp.any(match, axis=1)
-        gate = jnp.sum(jnp.where(match, gates[:, :, None], 0.0), axis=1)
-        lower = (jnp.arange(t)[:, None] >= jnp.arange(t)[None, :]).astype(bf16)
-        rank = jnp.dot(lower, hit.astype(bf16), preferred_element_type=f32).astype(jnp.int32) - 1
-        slot = jnp.where(hit & (rank < cap), rank, cap)
-        grow = (jnp.arange(nd)[:, None] == (jnp.arange(nd * half) // half)[None, :]).astype(bf16)
-        wide = lambda v: jnp.dot(v, grow, preferred_element_type=f32)
-        slots = wide(slot.astype(bf16))
-        g = sum(wide(part) for part in split3(gate))
-
-        moe = x.astype(f32)
-        for h in range(PARTS):
-            r = rx[h].reshape(nd * half, hd)
-            a1 = jnp.dot(r, w1[0], preferred_element_type=f32)
-            a3 = jnp.dot(r, w3[0], preferred_element_type=f32)
-            hh = (jax.nn.silu(a1) * a3).astype(bf16)
-            o = jnp.dot(hh, w2[0], preferred_element_type=f32)
-            peak = jnp.maximum(jnp.max(jnp.abs(o), axis=1), 1e-34)
-            o = (o * (FULL / peak)[:, None]).astype(f16)
-            back = lax.all_to_all(o.reshape(nd, half, hd), axes, 0, 0, tiled=True).reshape(nd * half, hd)
-            peak = lax.all_to_all(peak.reshape(nd, half), axes, 0, 0, tiled=True).reshape(1, nd * half)
-            mine = slots == (jnp.arange(nd * half) % half + h * half).astype(f32)[None, :]
-            wt = jnp.concatenate(split3(jnp.where(mine, g * (peak * (1.0 / FULL)), 0.0)), axis=0)
-            wt = lax.optimization_barrier(wt)
-            back = back.astype(f32)
-            hi = top8(back)
-            hi, lo = hi.astype(bf16), (back - hi).astype(bf16)
-            acc = jnp.dot(wt, hi, preferred_element_type=f32) + jnp.dot(wt, lo, preferred_element_type=f32)
-            moe = moe + (acc[:t] + acc[t:2 * t] + acc[2 * t:])
-        return moe.astype(bf16)
+        return experts(x, ids, gates, rx, w1[0], w3[0], w2[0])
 
     return jax.shard_map(local, mesh=mesh, in_specs=(tok, tok, tok, wsp, wsp, wsp),
                          out_specs=tok, check_vma=False)

time: 529 us -> 361 us (0.68)
  the two profiles are of different devices: /device:TPU:29 before, /device:TPU:1 now
where the time goes in v3:
time: 361 us; the launch traced here: 360 us
  Pallas kernels  353 us (98%)
  other arithmetic  4.4 us (1%)
    pallas_call x1, Pallas kernels, experts(): pl.pallas_call(functools.partial(experts_kernel, t, cap, groups), out_sha...  214 us
    pallas_call x1, Pallas kernels, dispatch(): pl.pallas_call(functools.partial(dispatch_kernel, t, cap, groups), out_sh...  139 us

profile of v3, /device:TPU:1, one launch (start us, length us, event | category | flops | bytes accessed | tf_op | source)
XLA Modules:
  0.0 359.5 jit_solution(3239575833487218700)
XLA Ops:
  0.0 0.8 convert_bitcast_fusion.1
  0.8 1.3 pad_maximum_fusion.1.info_ref
  2.1 2.3 pad_maximum_fusion.x_ref
  4.4 138.6 %dispatch.1.rx_ref = bf16[4,4,4,2,32,2048]{5,4,3,2,1,0:T(8,128)(2,1)} custom-call(bf16[264,2048]{1,0:T(8,128)(2,1)} %pad_maximum_fusion.x_ref), custom_call_target="tpu_custom_call" | custom-call | tf_op jit(solution)/shard_map/dispatch/pallas_call | solution.py:217
  143.0 214.2 %experts.1 = (bf16[256,2048]{1,0:T(8,128)(2,1)}, s16[3,4,4,8,32,768]{5,4,3,2,1,0:T(8,128)(2,1)}) custom-call(f32[16,256]{1,0:T(8,128)} %pad_maximum_fusion.1.info_ref, bf16[256,2048]{1,0:T(8,128)(2,1)} %x_ref.1, bf16[4,4,4,2,32,2048]{5,4,3,2,1,0:T(8,128)(2,1)} %dispatch.1.rx_ref, bf16[2048,768]{1,0:T(8,128)(2,1)} %bitcast.8, bf16[2048,768]{1,0:T(8,128)(2,1)} %bitcast.9, ...), custom_call_target="tpu_custom_call" | custom-call | tf_op jit(solution)/shard_map/experts/pallas_call | solution.py:569
  357.2 2.3 copy.10
  (3 shorter events, 0.0 us)

commit v4 on v3

--- a/solution.py
+++ b/solution.py
@@ -17,7 +17,8 @@
 STRIDES = (RING * RING * CORES, RING * CORES, CORES)
 RETURNS = ((2, 1, 0), (1, 0, 2), (0, 2, 1))
 TILE = 256
-SLOTS = 4
+WIDE = 512
+SLOTS = 5
 MESH = pl.DeviceIdType.MESH
 bf16, i16, f32 = jnp.bfloat16, jnp.int16, jnp.float32
 
@@ -31,7 +32,7 @@
     return list(zip(starts, widths))
 
 
-def dispatch_kernel(t, cap, groups, x_ref, rx_ref, got, out, upper, pick, load_sem, gsend, grecv, rsend, rrecv, self_sem):
+def dispatch_kernel(t, cap, groups, x_ref, ids_ref, rx_ref, got, out, upper, pick, load_sem, gsend, grecv, rsend, rrecv, self_sem):
     ey, ex, dp = lax.axis_index("ey"), lax.axis_index("ex"), lax.axis_index("dp")
     me = [ey // RING, ey % RING, ex // CORES]
     core = ex % CORES
@@ -49,8 +50,11 @@
     loads = []
     for g, (start, width) in enumerate(groups):
         loads.append(pltpu.make_async_copy(
-            x_ref.at[:, pl.ds(start, width)], got.at[g, 0, 0, :, pl.ds(0, width)], load_sem.at[g]))
-        loads[-1].start()
+            x_ref.at[:, pl.ds(start, width)], got.at[g, 0, 0, pl.ds(0, t), pl.ds(0, width)], load_sem.at[g, 0]))
+        loads.append(pltpu.make_async_copy(
+            ids_ref, got.at[g, 0, 0, pl.ds(t, IDROWS), pl.ds(0, t)], load_sem.at[g, 1]))
+    for load in loads:
+        load.start()
 
     barrier = pltpu.get_barrier_semaphore()
     peers = [(axis, by, dc) for axis in range(3) for by in range(1, RING) for dc in range(CORES)] + [(0, 0, 1)]
@@ -208,23 +212,19 @@
     t, hd = x.shape
     groups = column_groups(hd, 128)
     wide = max(w for _, w in groups)
-    tail = jnp.full((IDROWS, hd), -1.0, bf16)
-    for start, _ in groups:
-        tail = lax.dynamic_update_slice(tail, ids.T.astype(bf16), (0, start))
-    block = jnp.concatenate([x, tail], axis=0)
     n = len(groups)
     peers = RING * CORES
     return pl.pallas_call(
         functools.partial(dispatch_kernel, t, cap, groups),
         out_shape=jax.ShapeDtypeStruct((RING, RING, RING, CORES, cap, hd), bf16),
-        in_specs=[pl.BlockSpec(memory_space=pl.ANY)],
+        in_specs=[pl.BlockSpec(memory_space=pl.ANY)] * 2,
         out_specs=pl.BlockSpec(memory_space=pl.ANY),
         scratch_shapes=[
             pltpu.VMEM((n, RING, RING, t + IDROWS, wide), bf16),
             pltpu.VMEM((n, RING, peers, RING, cap, wide), bf16),
             pltpu.VMEM((t, t), bf16),
             pltpu.VMEM((peers * cap, t), bf16),
-            pltpu.SemaphoreType.DMA((n,)),
+            pltpu.SemaphoreType.DMA((n, 2)),
             pltpu.SemaphoreType.DMA((n, 4 + 4 * RING)),
             pltpu.SemaphoreType.DMA((n, 4 + 4 * RING)),
             pltpu.SemaphoreType.DMA((n, RING, peers)),
@@ -233,12 +233,12 @@
         ],
         compiler_params=pltpu.CompilerParams(collective_id=0, has_side_effects=True, vmem_limit_bytes=60 * 2 ** 20),
         name="dispatch",
-    )(block)
+    )(x, ids.T.astype(bf16))
 
 
 def experts_kernel(t, cap, groups, info_ref, x_ref, rx_ref, w1_ref, w3_ref, w2_ref, y_ref, r2,
-                   w1, w3, w2, xb, hh, res, ob, so, r1, s1, s2, acc, planes, info, db, wt, upper,
-                   wsem, xsem, isend, irecv, p1s, p1r, q1s, q1r, p2s, p2r, q2s, q2r, p3s, p3r, dsem):
+                   w1, w3, w2, xb, hh, res, top, ob, rest, so, r1, s1, s2, acc, planes, info, db, wt, upper, xv,
+                   wsem, xsem, isend, irecv, p1s, p1r, q1s, q1r, p2s, p2r, q2s, q2r, p3s, p3r, e1s, e1r, e2s, e2r, dsem):
     ey, ex, dp = lax.axis_index("ey"), lax.axis_index("ex"), lax.axis_index("dp")
     me = [ey // RING, ey % RING, ex // CORES]
     core = ex % CORES
@@ -247,6 +247,8 @@
     everyone = range(len(groups))
     col0 = [start for start, _ in groups]
     width = [w for _, w in groups]
+    main = min(width)
+    more = width[0] - main
     own = [me[RETURNS[g][0]] * CORES + core for g in everyone]
 
     def shifted(axis, by, c=None):
@@ -259,12 +261,14 @@
                                             device_id=to, device_id_type=MESH)
 
     loads = [pltpu.make_async_copy(a, b, wsem.at[n])
-             for n, (a, b) in enumerate(((w1_ref, w1), (w3_ref, w3), (w2_ref, w2)))]
-    for load in loads:
+             for n, (a, b) in enumerate(((w1_ref, w1), (w3_ref, w3), (w2_ref, w2), (x_ref, xv)))]
+    mine = [pltpu.make_async_copy(info_ref, info.at[axis, me[axis]], isend.at[axis, 0]) for axis in range(3)]
+    for load in mine + loads:
         load.start()
 
     def homes(step):
-        return (step + step // RING) % RING, step % RING
+        left = RING * RING - 1 - step
+        return (left + left // RING) % RING, left % RING
 
     def tile_load(step):
         dz, dy = homes(step)
@@ -279,8 +283,6 @@
     row = lax.broadcasted_iota(jnp.int32, (t, t), 0)
     col = lax.broadcasted_iota(jnp.int32, (t, t), 1)
     upper[...] = jnp.where(row <= col, 1.0, 0.0).astype(bf16)
-    for axis in range(3):
-        info[axis, me[axis]] = info_ref[...]
     pl.semaphore_wait(barrier, len(peers))
 
     told = []
@@ -289,7 +291,7 @@
             told.append(remote(info_ref, info.at[axis, me[axis]], isend.at[axis, by], irecv.at[axis, by], shifted(axis, by)))
             told[-1].start()
 
-    for load in loads:
+    for load in mine + loads[:3]:
         load.wait()
 
     def first(step):
@@ -301,8 +303,8 @@
             d, dc = n // CORES, n % CORES
             c = (core + dc) % CORES
             found.append((None, remote(
-                ob.at[slot, (me[2] + d) % RING, c, :, pl.ds(col0[0], width[0])],
-                r1.at[0, own[0], zh, yh, :, pl.ds(0, width[0])],
+                ob.at[slot, (me[2] + d) % RING, c, :, pl.ds(col0[0], main)],
+                r1.at[0, own[0], zh, yh, :, pl.ds(0, main)],
                 p1s.at[slot, n], p1r.at[0, n], shifted(2, d, c))))
         for g, axis, d, lead in ((1, 1, dy, zh), (2, 0, dz, yh)):
             for dc in range(CORES):
@@ -335,6 +337,8 @@
 
         tile_load(step).wait()
 
+        top[...] = jnp.zeros(top.shape, f32)
+
         def up(n, _):
             at = pl.ds(pl.multiple_of(n * TILE, TILE), TILE)
             xt = xb[step % 2].reshape(rows, hd)
@@ -345,13 +349,19 @@
 
         lax.fori_loop(0, ff // TILE, up, 0)
 
-        def down(n, peak):
-            at = pl.ds(pl.multiple_of(n * TILE, TILE), TILE)
+        def down(n, _):
+            at = pl.ds(pl.multiple_of(n * WIDE, WIDE), WIDE)
             o = jnp.dot(hh[...], w2[:, at], preferred_element_type=f32)
             res[:, at] = o
-            return jnp.maximum(peak, jnp.max(jnp.abs(o), axis=1, keepdims=True))
-
-        peak = lax.fori_loop(0, hd // TILE, down, jnp.full((rows, 1), 1e-30, f32))
+            o = jnp.abs(o)
+            most = o[:, 0:128]
+            for k in range(1, WIDE // 128):
+                most = jnp.maximum(most, o[:, k * 128:(k + 1) * 128])
+            top[...] = jnp.maximum(top[...], most)
+            return 0
+
+        lax.fori_loop(0, hd // WIDE, down, 0)
+        peak = jnp.maximum(jnp.max(top[...], axis=1, keepdims=True), 1e-30)
         for k in range(LINE):
             part = jnp.where(eye, peak[k * cap:(k + 1) * cap], 0.0)
             so[zh, yh, k // CORES, k % CORES] = jnp.sum(part, axis=0, keepdims=True) * (1.0 / FULL)
@@ -360,18 +370,20 @@
         def _():
             each(first(step - SLOTS), lambda copy: copy.wait_send())
 
-        factor = FULL / peak
+        top[...] = jnp.broadcast_to(FULL / peak, top.shape)
 
         def code(n, _):
-            at = pl.ds(pl.multiple_of(n * TILE, TILE), TILE)
-            v = jnp.round(res[:, at] * factor).astype(jnp.int32).astype(i16)
-            ob[slot, :, :, :, at] = v.reshape(RING, CORES, cap, TILE)
+            at = pl.ds(pl.multiple_of(n * 128, 128), 128)
+            v = jnp.round(res[:, at] * top[...]).astype(jnp.int32).astype(i16)
+            ob[slot, :, :, :, at] = v.reshape(RING, CORES, cap, 128)
             return 0
 
-        lax.fori_loop(0, hd // TILE, code, 0)
+        lax.fori_loop(0, hd // 128, code, 0)
         each(first(step), lambda copy: copy.start())
 
         r1[0, own[0], zh, yh, :, pl.ds(0, width[0])] = ob[slot, me[2], core, :, pl.ds(col0[0], width[0])]
+        if more:
+            rest[zh, yh] = ob[slot, :, :, :, pl.ds(col0[0] + main, more)]
         for g, d, lead in ((1, dy, zh), (2, dz, yh)):
             @pl.when(d == 0)
             def _():
@@ -380,6 +392,15 @@
         return 0
 
     lax.fori_loop(0, RING * RING, tile, 0)
+
+    later = []
+    if more:
+        for n in range(1, LINE):
+            d, dc = n // CORES, n % CORES
+            c = (core + dc) % CORES
+            later.append(remote(rest.at[:, :, (me[2] + d) % RING, c], r1.at[0, own[0], :, :, :, pl.ds(main, more)],
+                                e1s.at[n], e1r.at[n], shifted(2, d, c)))
+            later[-1].start()
 
     def scales(g, coord, c):
         return (so.at[:, :, coord, c], so.at[:, coord, :, c], so.at[coord, :, :, c])[g]
@@ -400,7 +421,7 @@
         for n in range(1, LINE):
             d, dc = n // CORES, n % CORES
             src = (me[axis] - d) % RING * CORES + (core + dc) % CORES
-            ref = r1.at[g, src, :, :, :, pl.ds(0, width[g])]
+            ref = r1.at[g, src, :, :, :, pl.ds(0, main)]
             pltpu.make_async_copy(ref, ref, p1r.at[g, n]).wait()
     for copy in hints:
         copy.wait_recv()
@@ -420,16 +441,29 @@
     def second(g, k3, d):
         _, axis, third = RETURNS[g]
         h3 = (me[third] + k3) % RING
-        src = (r1.at[0, :, h3, (me[axis] + d) % RING, :, pl.ds(0, width[0])] if g == 0 else
-               r1.at[1, :, (me[axis] + d) % RING, h3, :, pl.ds(0, width[1])] if g == 1 else
-               r1.at[2, :, h3, (me[axis] + d) % RING, :, pl.ds(0, width[2])])
-        return remote(src, r2.at[g, h3, me[axis], :, :, pl.ds(0, width[g])],
-                      p2s.at[g, k3, d], p2r.at[g, k3, d], shifted(axis, d))
+        at = pl.ds(0, main)
+        src = (r1.at[0, :, h3, (me[axis] + d) % RING, :, at] if g == 0 else
+               r1.at[1, :, (me[axis] + d) % RING, h3, :, at] if g == 1 else
+               r1.at[2, :, h3, (me[axis] + d) % RING, :, at])
+        return remote(src, r2.at[g, h3, me[axis], :, :, at], p2s.at[g, k3, d], p2r.at[g, k3, d], shifted(axis, d))
+
+    def second_more(k3, d):
+        _, axis, third = RETURNS[0]
+        h3 = (me[third] + k3) % RING
+        at = pl.ds(main, more)
+        return remote(r1.at[0, :, h3, (me[axis] + d) % RING, :, at], r2.at[0, h3, me[axis], :, :, at],
+                      e2s.at[k3, d], e2r.at[k3, d], shifted(axis, d))
 
     for k3 in (1, 2, 3, 0):
         for d in (1, 3, 2):
             for g in everyone:
                 second(g, k3, d).start()
+        if more and k3 == 1:
+            for copy in later:
+                copy.wait_recv()
+            for each_k3 in (1, 2, 3, 0):
+                for d in (1, 3, 2):
+                    second_more(each_k3, d).start()
 
     for copy in told:
         copy.wait_recv()
@@ -491,6 +525,8 @@
                 @pl.when(turn > 0)
                 def _():
                     second(g, k3, d).wait_recv()
+                    if more and g == 0:
+                        second_more(k3, d).wait_recv()
                     fetch(g).start()
 
             for g in everyone:
@@ -501,18 +537,20 @@
                 def _():
                     fetch(g).wait()
 
-                def piece(n, _):
-                    at = pl.ds(pl.multiple_of(n * TILE, TILE), TILE)
-                    q = db[g, :, :, at].reshape(rows, TILE).astype(f32)
+                def piece(at, size):
+                    q = db[g, :, :, at].reshape(rows, size).astype(f32)
                     high = q.astype(bf16)
                     low = (q - high.astype(f32)).astype(bf16)
                     dims = (((0,), (0,)), ((), ()))
                     p = (lax.dot_general(wt[...], high, dims, preferred_element_type=f32)
                          + lax.dot_general(wt[...], low, dims, preferred_element_type=f32))
                     acc[g, index, :, at] += p[0:t] + p[t:2 * t] + p[2 * t:]
-                    return 0
-
-                lax.fori_loop(0, width[g] // TILE, piece, 0)
+
+                begin = 0
+                while begin < width[g]:
+                    size = min(WIDE, width[g] - begin)
+                    piece(pl.ds(begin, size), size)
+                    begin += size
             return 0
 
         lax.fori_loop(0, RING, plane, 0)
@@ -530,16 +568,21 @@
 
     lax.fori_loop(0, RING, line, 0)
 
+    loads[3].wait()
     for g in everyone:
         for index in range(RING - 1):
             home(g, index).wait_recv()
-        for n in range(width[g] // TILE):
-            at = pl.ds(n * TILE, TILE)
-            to = pl.ds(col0[g] + n * TILE, TILE)
+
+        def finish(n, _):
+            at = pl.ds(pl.multiple_of(n * 128, 128), 128)
+            to = pl.ds(pl.multiple_of(col0[g] + n * 128, 128), 128)
             total = acc[g, RING - 1, :, at] + planes[g, 0, :, at] + planes[g, 1, :, at] + planes[g, 2, :, at]
-            y_ref[:, to] = (x_ref[:, to].astype(f32) + total).astype(bf16)
-
-    for copy in told + hints + moved:
+            y_ref[:, to] = (xv[:, to].astype(f32) + total).astype(bf16)
+            return 0
+
+        lax.fori_loop(0, width[g] // 128, finish, 0)
+
+    for copy in told + hints + moved + later:
         copy.wait_send()
 
     def last(step, _):
@@ -551,6 +594,8 @@
         for k3 in range(RING):
             for d in (1, 3, 2):
                 second(g, k3, d).wait_send()
+                if more and g == 0:
+                    second_more(k3, d).wait_send()
         for index in range(RING - 1):
             home(g, index).wait_send()
 
@@ -559,9 +604,10 @@
     t, hd = x.shape
     ff = w1.shape[1]
     cap = rx.shape[4]
-    groups = column_groups(hd, TILE)
+    groups = column_groups(hd, 128)
     wide = max(w for _, w in groups)
     n = len(groups)
+    more = max(wide - min(w for _, w in groups), 128)
     info = jnp.concatenate([ids.T.astype(f32), gates.T], axis=0)
     dma = pltpu.SemaphoreType.DMA
     anywhere = pl.BlockSpec(memory_space=pl.ANY)
@@ -570,14 +616,16 @@
         functools.partial(experts_kernel, t, cap, groups),
         out_shape=(jax.ShapeDtypeStruct((t, hd), bf16),
                    jax.ShapeDtypeStruct((n, RING, RING, LINE, cap, wide), i16)),
-        in_specs=[vmem, vmem] + [anywhere] * 4,
+        in_specs=[anywhere] * 6,
         out_specs=(vmem, anywhere),
         scratch_shapes=[
             pltpu.VMEM((hd, ff), bf16), pltpu.VMEM((hd, ff), bf16), pltpu.VMEM((ff, hd), bf16),
             pltpu.VMEM((2, RING, CORES, cap, hd), bf16),
             pltpu.VMEM((LINE * cap, ff), bf16),
             pltpu.VMEM((LINE * cap, hd), f32),
+            pltpu.VMEM((LINE * cap, 128), f32),
             pltpu.VMEM((SLOTS, RING, CORES, cap, hd), i16),
+            pltpu.VMEM((RING, RING, RING, CORES, cap, more), i16),
             pltpu.VMEM((RING, RING, RING, CORES, 1, 128), f32),
             pltpu.VMEM((n, LINE, RING, RING, cap, wide), i16),
             pltpu.VMEM((n, LINE, RING, RING, 1, 128), f32),
@@ -588,10 +636,11 @@
             pltpu.VMEM((n, LINE, cap, wide), i16),
             pltpu.VMEM((LINE * cap, 3 * t), bf16),
             pltpu.VMEM((t, t), bf16),
-            dma((3,)), dma((2,)), dma((3, RING)), dma((3, RING)),
+            pltpu.VMEM((t, hd), bf16),
+            dma((4,)), dma((2,)), dma((3, RING)), dma((3, RING)),
             dma((SLOTS, LINE + 4)), dma((n, LINE)), dma((n, LINE)), dma((n, LINE)),
             dma((n, RING, RING)), dma((n, RING, RING)), dma((n, RING)), dma((n, RING)),
-            dma((n, RING)), dma((n, RING)), dma((n,)),
+            dma((n, RING)), dma((n, RING)), dma((LINE,)), dma((LINE,)), dma((RING, RING)), dma((RING, RING)), dma((n,)),
         ],
         compiler_params=pltpu.CompilerParams(collective_id=1, has_side_effects=True, vmem_limit_bytes=67043328),
         name="experts",

time: 361 us -> 339 us (0.939)
  Pallas kernels: 353 us -> 334 us
    pallas_call x1, Pallas kernels: 214 us -> 195 us  [experts(): pl.pallas_call(functools.partial(experts_kernel, t, cap, groups), out_sha...]
where the time goes in v4:
time: 339 us
  Pallas kernels  334 us (99%)
    pallas_call x1, Pallas kernels, experts(): pl.pallas_call(functools.partial(experts_kernel, t, cap, groups), out_sha...  195 us
    pallas_call x1, Pallas kernels, dispatch(): pl.pallas_call(functools.partial(dispatch_kernel, t, cap, groups), out_sh...  139 us

profile of v4, /device:TPU:1, one launch (start us, length us, event | category | flops | bytes accessed | tf_op | source)
XLA Modules:
  0.0 338.6 jit_solution(17169750773334878016)
XLA Ops:
  0.0 1.4 convert_bitcast_fusion.1
  1.4 1.3 pad_maximum_fusion.info_ref
  2.7 138.6 %dispatch.1.rx_ref = bf16[4,4,4,2,32,2048]{5,4,3,2,1,0:T(8,128)(2,1)} custom-call(bf16[256,2048]{1,0:T(8,128)(2,1)} %x_ref.3, bf16[8,256]{1,0:T(8,128)(2,1)} %get-tuple-element.7.ids_ref), custom_call_target="tpu_custom_call" | custom-call | tf_op jit(solution)/shard_map/dispatch/pallas_call | solution.py:217
  141.3 195.0 %experts.1 = (bf16[256,2048]{1,0:T(8,128)(2,1)}, s16[3,4,4,8,32,768]{5,4,3,2,1,0:T(8,128)(2,1)}) custom-call(f32[16,256]{1,0:T(8,128)} %pad_maximum_fusion.info_ref, bf16[256,2048]{1,0:T(8,128)(2,1)} %x_ref.3, bf16[4,4,4,2,32,2048]{5,4,3,2,1,0:T(8,128)(2,1)} %dispatch.1.rx_ref, bf16[2048,768]{1,0:T(8,128)(2,1)} %bitcast.8, bf16[2048,768]{1,0:T(8,128)(2,1)} %bitcast.9, ...), custom_call_target="tpu_custom_call" | custom-call | tf_op jit(solution)/shard_map/experts/pallas_call | solution.py:615
  336.3 2.3 copy.8

commit v5 on v4

--- a/solution.py
+++ b/solution.py
@@ -393,6 +393,20 @@
 
     lax.fori_loop(0, RING * RING, tile, 0)
 
+    def scales(g, coord, c):
+        return (so.at[:, :, coord, c], so.at[:, coord, :, c], so.at[coord, :, :, c])[g]
+
+    hints = []
+    for g in everyone:
+        axis = RETURNS[g][0]
+        s1[g, own[g]] = (so[:, :, me[2], core], so[:, me[1], :, core], so[me[0], :, :, core])[g]
+        for n in range(1, LINE):
+            d, dc = n // CORES, n % CORES
+            c = (core + dc) % CORES
+            hints.append(remote(scales(g, (me[axis] + d) % RING, c), s1.at[g, own[g]],
+                                q1s.at[g, n], q1r.at[g, n], shifted(axis, d, c)))
+            hints[-1].start()
+
     later = []
     if more:
         for n in range(1, LINE):
@@ -402,41 +416,8 @@
                                 e1s.at[n], e1r.at[n], shifted(2, d, c)))
             later[-1].start()
 
-    def scales(g, coord, c):
-        return (so.at[:, :, coord, c], so.at[:, coord, :, c], so.at[coord, :, :, c])[g]
-
-    hints = []
-    for g in everyone:
-        axis = RETURNS[g][0]
-        s1[g, own[g]] = (so[:, :, me[2], core], so[:, me[1], :, core], so[me[0], :, :, core])[g]
-        for n in range(1, LINE):
-            d, dc = n // CORES, n % CORES
-            c = (core + dc) % CORES
-            hints.append(remote(scales(g, (me[axis] + d) % RING, c), s1.at[g, own[g]],
-                                q1s.at[g, n], q1r.at[g, n], shifted(axis, d, c)))
-            hints[-1].start()
-
-    for g in everyone:
-        axis = RETURNS[g][0]
-        for n in range(1, LINE):
-            d, dc = n // CORES, n % CORES
-            src = (me[axis] - d) % RING * CORES + (core + dc) % CORES
-            ref = r1.at[g, src, :, :, :, pl.ds(0, main)]
-            pltpu.make_async_copy(ref, ref, p1r.at[g, n]).wait()
-    for copy in hints:
-        copy.wait_recv()
-
     def lane(ref, g, h2, h3):
         return (ref.at[0, :, h3, h2], ref.at[1, :, h2, h3], ref.at[2, :, h3, h2])[g]
-
-    moved = []
-    for g in everyone:
-        axis = RETURNS[g][1]
-        s2[g, me[axis]] = (s1[0, :, :, me[1]], s1[1, :, me[0]], s1[2, :, :, me[2]])[g]
-        for d in (1, 3, 2):
-            moved.append(remote(lane(s1, g, (me[axis] + d) % RING, slice(None)), s2.at[g, me[axis]],
-                                q2s.at[g, d], q2r.at[g, d], shifted(axis, d)))
-            moved[-1].start()
 
     def second(g, k3, d):
         _, axis, third = RETURNS[g]
@@ -454,16 +435,36 @@
         return remote(r1.at[0, :, h3, (me[axis] + d) % RING, :, at], r2.at[0, h3, me[axis], :, :, at],
                       e2s.at[k3, d], e2r.at[k3, d], shifted(axis, d))
 
+    for g in everyone:
+        axis = RETURNS[g][0]
+        for n in range(1, LINE):
+            d, dc = n // CORES, n % CORES
+            src = (me[axis] - d) % RING * CORES + (core + dc) % CORES
+            ref = r1.at[g, src, :, :, :, pl.ds(0, main)]
+            pltpu.make_async_copy(ref, ref, p1r.at[g, n]).wait()
+        for d in (1, 3, 2):
+            second(g, 1, d).start()
+
+    for copy in hints:
+        copy.wait_recv()
+    moved = []
+    for g in everyone:
+        axis = RETURNS[g][1]
+        s2[g, me[axis]] = (s1[0, :, :, me[1]], s1[1, :, me[0]], s1[2, :, :, me[2]])[g]
+        for d in (1, 3, 2):
+            moved.append(remote(lane(s1, g, (me[axis] + d) % RING, slice(None)), s2.at[g, me[axis]],
+                                q2s.at[g, d], q2r.at[g, d], shifted(axis, d)))
+            moved[-1].start()
+
+    for copy in later:
+        copy.wait_recv()
     for k3 in (1, 2, 3, 0):
         for d in (1, 3, 2):
+            if more:
+                second_more(k3, d).start()
             for g in everyone:
-                second(g, k3, d).start()
-        if more and k3 == 1:
-            for copy in later:
-                copy.wait_recv()
-            for each_k3 in (1, 2, 3, 0):
-                for d in (1, 3, 2):
-                    second_more(each_k3, d).start()
+                if k3 != 1:
+                    second(g, k3, d).start()
 
     for copy in told:
         copy.wait_recv()
@@ -551,14 +552,14 @@
                     size = min(WIDE, width[g] - begin)
                     piece(pl.ds(begin, size), size)
                     begin += size
+
+                @pl.when((turn == RING - 1) & (index < RING - 1))
+                def _():
+                    home(g, index).start()
             return 0
 
         lax.fori_loop(0, RING, plane, 0)
 
-        @pl.when(index < RING - 1)
-        def _():
-            for g in everyone:
-                home(g, index).start()
         return 0
 
     def home(g, index):

time: 339 us -> 328 us (0.968)
  Pallas kernels: 334 us -> 322 us
    pallas_call x1, Pallas kernels: 195 us -> 183 us  [experts(): pl.pallas_call(functools.partial(experts_kernel, t, cap, groups), out_sha...]
where the time goes in v5:
time: 328 us; the launch traced here: 327 us
  Pallas kernels  322 us (98%)
    pallas_call x1, Pallas kernels, experts(): pl.pallas_call(functools.partial(experts_kernel, t, cap, groups), out_sha...  183 us
    pallas_call x1, Pallas kernels, dispatch(): pl.pallas_call(functools.partial(dispatch_kernel, t, cap, groups), out_sh...  139 us

profile of v5, /device:TPU:1, one launch (start us, length us, event | category | flops | bytes accessed | tf_op | source)
XLA Modules:
  0.0 327.1 jit_solution(726858923692678940)
XLA Ops:
  0.0 1.4 convert_bitcast_fusion.1
  1.4 1.3 pad_maximum_fusion.info_ref
  2.7 138.6 %dispatch.1.rx_ref = bf16[4,4,4,2,32,2048]{5,4,3,2,1,0:T(8,128)(2,1)} custom-call(bf16[256,2048]{1,0:T(8,128)(2,1)} %x_ref.3, bf16[8,256]{1,0:T(8,128)(2,1)} %get-tuple-element.7.ids_ref), custom_call_target="tpu_custom_call" | custom-call | tf_op jit(solution)/shard_map/dispatch/pallas_call | solution.py:217
  141.3 183.5 %experts.1 = (bf16[256,2048]{1,0:T(8,128)(2,1)}, s16[3,4,4,8,32,768]{5,4,3,2,1,0:T(8,128)(2,1)}) custom-call(f32[16,256]{1,0:T(8,128)} %pad_maximum_fusion.info_ref, bf16[256,2048]{1,0:T(8,128)(2,1)} %x_ref.3, bf16[4,4,4,2,32,2048]{5,4,3,2,1,0:T(8,128)(2,1)} %dispatch.1.rx_ref, bf16[2048,768]{1,0:T(8,128)(2,1)} %bitcast.8, bf16[2048,768]{1,0:T(8,128)(2,1)} %bitcast.9, ...), custom_call_target="tpu_custom_call" | custom-call | tf_op jit(solution)/shard_map/experts/pallas_call | solution.py:616
  324.8 2.3 copy.8

commit v6 on v5

--- a/solution.py
+++ b/solution.py
@@ -17,6 +17,7 @@
 STRIDES = (RING * RING * CORES, RING * CORES, CORES)
 RETURNS = ((2, 1, 0), (1, 0, 2), (0, 2, 1))
 TILE = 256
+LINES = (2, 1, 3, 0)
 WIDE = 512
 SLOTS = 5
 MESH = pl.DeviceIdType.MESH
@@ -237,8 +238,8 @@
 
 
 def experts_kernel(t, cap, groups, info_ref, x_ref, rx_ref, w1_ref, w3_ref, w2_ref, y_ref, r2,
-                   w1, w3, w2, xb, hh, res, top, ob, rest, so, r1, s1, s2, acc, planes, info, db, wt, upper, xv,
-                   wsem, xsem, isend, irecv, p1s, p1r, q1s, q1r, p2s, p2r, q2s, q2r, p3s, p3r, e1s, e1r, e2s, e2r, dsem):
+                   w1, w3, w2, xb, hh, res, top, ob, rest, so, r1, s1, s2, acc, part, planes, info, db, wt, upper, xv,
+                   wsem, xsem, isend, irecv, p1s, p1r, q1s, q1r, p2s, p2r, q2s, q2r, p3s, p3r, hs, hr, e1s, e1r, e2s, e2r, dsem):
     ey, ex, dp = lax.axis_index("ey"), lax.axis_index("ex"), lax.axis_index("dp")
     me = [ey // RING, ey % RING, ex // CORES]
     core = ex % CORES
@@ -326,61 +327,23 @@
 
     eye = lax.broadcasted_iota(jnp.int32, (cap, 128), 0) == lax.broadcasted_iota(jnp.int32, (cap, 128), 1)
 
-    def tile(step, _):
+    def code(step, begin, end):
+        slot = step % SLOTS
+        for n in range(begin, end):
+            at = pl.ds(n * 128, 128)
+            v = jnp.round(res[:, at] * top[...]).astype(jnp.int32).astype(i16)
+            ob[slot, :, :, :, at] = v.reshape(RING, CORES, cap, 128)
+
+    def room(step):
+        @pl.when(step >= SLOTS)
+        def _():
+            each(first(step - SLOTS), lambda copy: copy.wait_send())
+
+    def leave(step):
+        each(first(step), lambda copy: copy.start())
         dz, dy = homes(step)
         zh, yh = (me[0] + dz) % RING, (me[1] + dy) % RING
         slot = step % SLOTS
-
-        @pl.when(step + 1 < RING * RING)
-        def _():
-            tile_load(step + 1).start()
-
-        tile_load(step).wait()
-
-        top[...] = jnp.zeros(top.shape, f32)
-
-        def up(n, _):
-            at = pl.ds(pl.multiple_of(n * TILE, TILE), TILE)
-            xt = xb[step % 2].reshape(rows, hd)
-            a1 = jnp.dot(xt, w1[:, at], preferred_element_type=f32)
-            a3 = jnp.dot(xt, w3[:, at], preferred_element_type=f32)
-            hh[:, at] = (a1 * (1.0 / (1.0 + jnp.exp(-a1))) * a3).astype(bf16)
-            return 0
-
-        lax.fori_loop(0, ff // TILE, up, 0)
-
-        def down(n, _):
-            at = pl.ds(pl.multiple_of(n * WIDE, WIDE), WIDE)
-            o = jnp.dot(hh[...], w2[:, at], preferred_element_type=f32)
-            res[:, at] = o
-            o = jnp.abs(o)
-            most = o[:, 0:128]
-            for k in range(1, WIDE // 128):
-                most = jnp.maximum(most, o[:, k * 128:(k + 1) * 128])
-            top[...] = jnp.maximum(top[...], most)
-            return 0
-
-        lax.fori_loop(0, hd // WIDE, down, 0)
-        peak = jnp.maximum(jnp.max(top[...], axis=1, keepdims=True), 1e-30)
-        for k in range(LINE):
-            part = jnp.where(eye, peak[k * cap:(k + 1) * cap], 0.0)
-            so[zh, yh, k // CORES, k % CORES] = jnp.sum(part, axis=0, keepdims=True) * (1.0 / FULL)
-
-        @pl.when(step >= SLOTS)
-        def _():
-            each(first(step - SLOTS), lambda copy: copy.wait_send())
-
-        top[...] = jnp.broadcast_to(FULL / peak, top.shape)
-
-        def code(n, _):
-            at = pl.ds(pl.multiple_of(n * 128, 128), 128)
-            v = jnp.round(res[:, at] * top[...]).astype(jnp.int32).astype(i16)
-            ob[slot, :, :, :, at] = v.reshape(RING, CORES, cap, 128)
-            return 0
-
-        lax.fori_loop(0, hd // 128, code, 0)
-        each(first(step), lambda copy: copy.start())
-
         r1[0, own[0], zh, yh, :, pl.ds(0, width[0])] = ob[slot, me[2], core, :, pl.ds(col0[0], width[0])]
         if more:
             rest[zh, yh] = ob[slot, :, :, :, pl.ds(col0[0] + main, more)]
@@ -389,9 +352,49 @@
             def _():
                 for xh in range(RING):
                     r1[g, own[g], lead, xh, :, pl.ds(0, width[g])] = ob[slot, xh, core, :, pl.ds(col0[g], width[g])]
+
+    def tile(step, _):
+        dz, dy = homes(step)
+        zh, yh = (me[0] + dz) % RING, (me[1] + dy) % RING
+
+        @pl.when(step + 1 < RING * RING)
+        def _():
+            tile_load(step + 1).start()
+
+        room(step - 1)
+        tile_load(step).wait()
+        ups, codes = ff // TILE, hd // 128
+        for n in range(ups):
+            at = pl.ds(n * TILE, TILE)
+            xt = xb[step % 2].reshape(rows, hd)
+            a1 = jnp.dot(xt, w1[:, at], preferred_element_type=f32)
+            a3 = jnp.dot(xt, w3[:, at], preferred_element_type=f32)
+            hh[:, at] = (a1 * (1.0 / (1.0 + jnp.exp(-a1))) * a3).astype(bf16)
+            code(step - 1, codes * n // ups, codes * (n + 1) // ups)
+
+        @pl.when(step > 0)
+        def _():
+            leave(step - 1)
+
+        most = jnp.zeros((rows, 128), f32)
+        for n in range(hd // WIDE):
+            o = jnp.dot(hh[...], w2[:, n * WIDE:(n + 1) * WIDE], preferred_element_type=f32)
+            res[:, n * WIDE:(n + 1) * WIDE] = o
+            o = jnp.abs(o)
+            for k in range(WIDE // 128):
+                most = jnp.maximum(most, o[:, k * 128:(k + 1) * 128])
+        peak = jnp.maximum(jnp.max(most, axis=1, keepdims=True), 1e-30)
+        top[...] = jnp.broadcast_to(FULL / peak, top.shape)
+        for k in range(LINE):
+            part = jnp.where(eye, peak[k * cap:(k + 1) * cap], 0.0)
+            so[zh, yh, k // CORES, k % CORES] = jnp.sum(part, axis=0, keepdims=True) * (1.0 / FULL)
         return 0
 
-    lax.fori_loop(0, RING * RING, tile, 0)
+    steps = RING * RING
+    lax.fori_loop(0, steps, tile, 0)
+    room(steps - 1)
+    code(steps - 1, 0, hd // 128)
+    leave(steps - 1)
 
     def scales(g, coord, c):
         return (so.at[:, :, coord, c], so.at[:, coord, :, c], so.at[coord, :, :, c])[g]
@@ -443,7 +446,7 @@
             ref = r1.at[g, src, :, :, :, pl.ds(0, main)]
             pltpu.make_async_copy(ref, ref, p1r.at[g, n]).wait()
         for d in (1, 3, 2):
-            second(g, 1, d).start()
+            second(g, LINES[0], d).start()
 
     for copy in hints:
         copy.wait_recv()
@@ -458,13 +461,16 @@
 
     for copy in later:
         copy.wait_recv()
-    for k3 in (1, 2, 3, 0):
+    def rest_of(k3):
         for d in (1, 3, 2):
             if more:
                 second_more(k3, d).start()
             for g in everyone:
-                if k3 != 1:
+                if k3 != LINES[0]:
                     second(g, k3, d).start()
+
+    for k3 in LINES[:-1]:
+        rest_of(k3)
 
     for copy in told:
         copy.wait_recv()
@@ -499,7 +505,7 @@
             wt[at, pl.ds(2 * t, t)] = w.astype(bf16)
 
     def line(index, _):
-        k3 = (index + 1) % RING
+        k3 = 2 - index + 3 * (index // 2) - 2 * (index // 3)
 
         def plane(turn, _):
             d = turn + turn // 2 - 2 * (turn // 3)
@@ -553,31 +559,50 @@
                     piece(pl.ds(begin, size), size)
                     begin += size
 
-                @pl.when((turn == RING - 1) & (index < RING - 1))
+                @pl.when((turn == RING - 1) & (index == 0))
                 def _():
-                    home(g, index).start()
+                    for way in range(2):
+                        opposite(g, way).start()
+
+                @pl.when((turn == RING - 1) & (index == 2))
+                def _():
+                    for way in range(2):
+                        opposite(g, way).wait_recv()
+                        rows_of = pl.ds(way * (t // 2), t // 2)
+                        at = pl.ds(0, width[g])
+                        acc[g, 1 + way, rows_of, at] += part[g, way, :, at]
+                    for way in range(2):
+                        home(g, way).start()
             return 0
 
         lax.fori_loop(0, RING, plane, 0)
 
+        @pl.when(index == 0)
+        def _():
+            rest_of(LINES[-1])
         return 0
 
-    def home(g, index):
+    def opposite(g, way):
         at = pl.ds(0, width[g])
-        return remote(acc.at[g, index, :, at], planes.at[g, index, :, at],
-                      p3s.at[g, index], p3r.at[g, index], shifted(RETURNS[g][2], (index + 1) % RING))
+        return remote(acc.at[g, 0, pl.ds(way * (t // 2), t // 2), at], part.at[g, way, :, at],
+                      hs.at[g, way], hr.at[g, way], shifted(RETURNS[g][2], LINES[1 + way]))
+
+    def home(g, way):
+        at = pl.ds(0, width[g])
+        return remote(acc.at[g, 1 + way, :, at], planes.at[g, way, :, at],
+                      p3s.at[g, way], p3r.at[g, way], shifted(RETURNS[g][2], LINES[1 + way]))
 
     lax.fori_loop(0, RING, line, 0)
 
     loads[3].wait()
     for g in everyone:
-        for index in range(RING - 1):
-            home(g, index).wait_recv()
+        for way in range(2):
+            home(g, way).wait_recv()
 
         def finish(n, _):
             at = pl.ds(pl.multiple_of(n * 128, 128), 128)
             to = pl.ds(pl.multiple_of(col0[g] + n * 128, 128), 128)
-            total = acc[g, RING - 1, :, at] + planes[g, 0, :, at] + planes[g, 1, :, at] + planes[g, 2, :, at]
+            total = acc[g, RING - 1, :, at] + planes[g, 0, :, at] + planes[g, 1, :, at]
             y_ref[:, to] = (xv[:, to].astype(f32) + total).astype(bf16)
             return 0
 
@@ -597,8 +622,9 @@
                 second(g, k3, d).wait_send()
                 if more and g == 0:
                     second_more(k3, d).wait_send()
-        for index in range(RING - 1):
-            home(g, index).wait_send()
+        for way in range(2):
+            opposite(g, way).wait_send()
+            home(g, way).wait_send()
 
 
 def experts(x, ids, gates, rx, w1, w3, w2):
@@ -632,7 +658,8 @@
             pltpu.VMEM((n, LINE, RING, RING, 1, 128), f32),
             pltpu.VMEM((n, RING, LINE, RING, 1, 128), f32),
             pltpu.VMEM((n, RING, t, wide), f32),
-            pltpu.VMEM((n, RING - 1, t, wide), f32),
+            pltpu.VMEM((n, 2, t // 2, wide), f32),
+            pltpu.VMEM((n, 2, t, wide), f32),
             pltpu.VMEM((3, RING, 16, t), f32),
             pltpu.VMEM((n, LINE, cap, wide), i16),
             pltpu.VMEM((LINE * cap, 3 * t), bf16),
@@ -641,7 +668,7 @@
             dma((4,)), dma((2,)), dma((3, RING)), dma((3, RING)),
             dma((SLOTS, LINE + 4)), dma((n, LINE)), dma((n, LINE)), dma((n, LINE)),
             dma((n, RING, RING)), dma((n, RING, RING)), dma((n, RING)), dma((n, RING)),
-            dma((n, RING)), dma((n, RING)), dma((LINE,)), dma((LINE,)), dma((RING, RING)), dma((RING, RING)), dma((n,)),
+            dma((n, 2)), dma((n, 2)), dma((n, 2)), dma((n, 2)), dma((LINE,)), dma((LINE,)), dma((RING, RING)), dma((RING, RING)), dma((n,)),
         ],
         compiler_params=pltpu.CompilerParams(collective_id=1, has_side_effects=True, vmem_limit_bytes=67043328),
         name="experts",

time: 328 us -> 313 us (0.954)
  Pallas kernels: 322 us -> 308 us
    pallas_call x1, Pallas kernels: 183 us -> 169 us  [experts(): pl.pallas_call(functools.partial(experts_kernel, t, cap, groups), out_sha...]
where the time goes in v6:
time: 313 us
  Pallas kernels  308 us (98%)
    pallas_call x1, Pallas kernels, experts(): pl.pallas_call(functools.partial(experts_kernel, t, cap, groups), out_sha...  169 us
    pallas_call x1, Pallas kernels, dispatch(): pl.pallas_call(functools.partial(dispatch_kernel, t, cap, groups), out_sh...  139 us

profile of v6, /device:TPU:1, one launch (start us, length us, event | category | flops | bytes accessed | tf_op | source)
XLA Modules:
  0.0 312.8 jit_solution(14775393942111132337)
XLA Ops:
  0.0 1.4 convert_bitcast_fusion.1
  1.4 1.3 pad_maximum_fusion.info_ref
  2.7 138.6 %dispatch.1.rx_ref = bf16[4,4,4,2,32,2048]{5,4,3,2,1,0:T(8,128)(2,1)} custom-call(bf16[256,2048]{1,0:T(8,128)(2,1)} %x_ref.3, bf16[8,256]{1,0:T(8,128)(2,1)} %get-tuple-element.7.ids_ref), custom_call_target="tpu_custom_call" | custom-call | tf_op jit(solution)/shard_map/dispatch/pallas_call | solution.py:218
  141.3 169.2 %experts.1 = (bf16[256,2048]{1,0:T(8,128)(2,1)}, s16[3,4,4,8,32,768]{5,4,3,2,1,0:T(8,128)(2,1)}) custom-call(f32[16,256]{1,0:T(8,128)} %pad_maximum_fusion.info_ref, bf16[256,2048]{1,0:T(8,128)(2,1)} %x_ref.3, bf16[4,4,4,2,32,2048]{5,4,3,2,1,0:T(8,128)(2,1)} %dispatch.1.rx_ref, bf16[2048,768]{1,0:T(8,128)(2,1)} %bitcast.8, bf16[2048,768]{1,0:T(8,128)(2,1)} %bitcast.9, ...), custom_call_target="tpu_custom_call" | custom-call | tf_op jit(solution)/shard_map/experts/pallas_call | solution.py:642
  310.5 2.3 copy.8

commit v7 on v6

--- a/solution.py
+++ b/solution.py
@@ -21,6 +21,7 @@
 WIDE = 512
 SLOTS = 5
 MESH = pl.DeviceIdType.MESH
+PEERS = [(axis, by, dc) for axis in range(3) for by in range(1, RING) for dc in range(CORES)] + [(0, 0, 1)]
 bf16, i16, f32 = jnp.bfloat16, jnp.int16, jnp.float32
 
 
@@ -33,7 +34,8 @@
     return list(zip(starts, widths))
 
 
-def dispatch_kernel(t, cap, groups, x_ref, ids_ref, rx_ref, got, out, upper, pick, load_sem, gsend, grecv, rsend, rrecv, self_sem):
+def dispatch_part(t, cap, groups, x_ref, rx_ref, idv, gatev, upper, info, load_sem, gsend, grecv, rsend, rrecv, self_sem,
+                  isend, irecv, weight_loads, got, out, pick):
     ey, ex, dp = lax.axis_index("ey"), lax.axis_index("ex"), lax.axis_index("dp")
     me = [ey // RING, ey % RING, ex // CORES]
     core = ex % CORES
@@ -48,24 +50,24 @@
         coords[axis] = (coords[axis] + by) % RING
         return device(coords, core if c is None else c)
 
-    loads = []
-    for g, (start, width) in enumerate(groups):
-        loads.append(pltpu.make_async_copy(
-            x_ref.at[:, pl.ds(start, width)], got.at[g, 0, 0, pl.ds(0, t), pl.ds(0, width)], load_sem.at[g, 0]))
-        loads.append(pltpu.make_async_copy(
-            ids_ref, got.at[g, 0, 0, pl.ds(t, IDROWS), pl.ds(0, t)], load_sem.at[g, 1]))
+    loads = [pltpu.make_async_copy(x_ref.at[:, pl.ds(start, width)], got.at[g, 0, 0, pl.ds(0, t), pl.ds(0, width)],
+                                   load_sem.at[g]) for g, (start, width) in enumerate(groups)]
     for load in loads:
         load.start()
 
     barrier = pltpu.get_barrier_semaphore()
-    peers = [(axis, by, dc) for axis in range(3) for by in range(1, RING) for dc in range(CORES)] + [(0, 0, 1)]
-    for axis, by, dc in peers:
-        pl.semaphore_signal(barrier, inc=1, device_id=shifted(axis, by, (core + dc) % CORES),
-                            device_id_type=MESH)
+    for axis, by, dc in PEERS:
+        pl.semaphore_signal(barrier, inc=1, device_id=shifted(axis, by, (core + dc) % CORES), device_id_type=MESH)
     row = lax.broadcasted_iota(jnp.int32, (t, t), 0)
     col = lax.broadcasted_iota(jnp.int32, (t, t), 1)
     upper[...] = jnp.where(row <= col, 1.0, 0.0).astype(bf16)
-    pl.semaphore_wait(barrier, len(peers))
+    ids = idv[...].astype(f32)
+    for g in range(len(groups)):
+        got[g, 0, 0, pl.ds(t, IDROWS), pl.ds(0, t)] = ids.astype(bf16)
+    for axis in range(3):
+        info[axis, me[axis], 0:8, :] = ids
+        info[axis, me[axis], 8:16, :] = gatev[...]
+    pl.semaphore_wait(barrier, len(PEERS))
     for load in loads:
         load.wait()
 
@@ -104,6 +106,8 @@
     for g in everyone:
         first(g)
         second(g, 0)
+    for load in weight_loads:
+        load.start()
     for g in everyone:
         p = ORDERS[g][0]
         hops[g, 0].wait_recv()
@@ -199,47 +203,29 @@
         choose(g, 2)
         exchange(g, 2)
 
+    told = []
+    for axis in range(3):
+        for by in range(1, RING):
+            told.append(pltpu.make_async_remote_copy(
+                src_ref=info.at[axis, me[axis]], dst_ref=info.at[axis, me[axis]], send_sem=isend.at[axis, by],
+                recv_sem=irecv.at[axis, by], device_id=shifted(axis, by), device_id_type=MESH))
+            told[-1].start()
+
     for copy in sends:
         copy.wait_recv()
     for copy in keeps:
         copy.wait()
     for copy in hops.values():
         copy.wait_send()
-    for copy in sends:
+    for copy in sends + told:
         copy.wait_send()
-
-
-def dispatch(x, ids, cap):
-    t, hd = x.shape
-    groups = column_groups(hd, 128)
-    wide = max(w for _, w in groups)
-    n = len(groups)
-    peers = RING * CORES
-    return pl.pallas_call(
-        functools.partial(dispatch_kernel, t, cap, groups),
-        out_shape=jax.ShapeDtypeStruct((RING, RING, RING, CORES, cap, hd), bf16),
-        in_specs=[pl.BlockSpec(memory_space=pl.ANY)] * 2,
-        out_specs=pl.BlockSpec(memory_space=pl.ANY),
-        scratch_shapes=[
-            pltpu.VMEM((n, RING, RING, t + IDROWS, wide), bf16),
-            pltpu.VMEM((n, RING, peers, RING, cap, wide), bf16),
-            pltpu.VMEM((t, t), bf16),
-            pltpu.VMEM((peers * cap, t), bf16),
-            pltpu.SemaphoreType.DMA((n, 2)),
-            pltpu.SemaphoreType.DMA((n, 4 + 4 * RING)),
-            pltpu.SemaphoreType.DMA((n, 4 + 4 * RING)),
-            pltpu.SemaphoreType.DMA((n, RING, peers)),
-            pltpu.SemaphoreType.DMA((n, RING, peers)),
-            pltpu.SemaphoreType.DMA((n, RING)),
-        ],
-        compiler_params=pltpu.CompilerParams(collective_id=0, has_side_effects=True, vmem_limit_bytes=60 * 2 ** 20),
-        name="dispatch",
-    )(x, ids.T.astype(bf16))
-
-
-def experts_kernel(t, cap, groups, info_ref, x_ref, rx_ref, w1_ref, w3_ref, w2_ref, y_ref, r2,
-                   w1, w3, w2, xb, hh, res, top, ob, rest, so, r1, s1, s2, acc, part, planes, info, db, wt, upper, xv,
-                   wsem, xsem, isend, irecv, p1s, p1r, q1s, q1r, p2s, p2r, q2s, q2r, p3s, p3r, hs, hr, e1s, e1r, e2s, e2r, dsem):
+    for copy in told:
+        copy.wait_recv()
+
+
+def experts_part(t, cap, groups, x_ref, rx_ref, y_ref, r2, w1, w3, w2, info, upper, ready, weight_loads, xload_sem, sems,
+                 xb, hh, res, top, ob, rest, so, r1, s1, s2, acc, part, planes, db, wt, xv):
+    xsem, p1s, p1r, q1s, q1r, p2s, p2r, q2s, q2r, p3s, p3r, hs, hr, e1s, e1r, e2s, e2r, dsem = sems
     ey, ex, dp = lax.axis_index("ey"), lax.axis_index("ex"), lax.axis_index("dp")
     me = [ey // RING, ey % RING, ex // CORES]
     core = ex % CORES
@@ -261,12 +247,6 @@
         return pltpu.make_async_remote_copy(src_ref=src, dst_ref=dst, send_sem=send, recv_sem=recv,
                                             device_id=to, device_id_type=MESH)
 
-    loads = [pltpu.make_async_copy(a, b, wsem.at[n])
-             for n, (a, b) in enumerate(((w1_ref, w1), (w3_ref, w3), (w2_ref, w2), (x_ref, xv)))]
-    mine = [pltpu.make_async_copy(info_ref, info.at[axis, me[axis]], isend.at[axis, 0]) for axis in range(3)]
-    for load in mine + loads:
-        load.start()
-
     def homes(step):
         left = RING * RING - 1 - step
         return (left + left // RING) % RING, left % RING
@@ -277,22 +257,11 @@
 
     tile_load(0).start()
 
-    barrier = pltpu.get_barrier_semaphore()
-    peers = [(axis, by, dc) for axis in range(3) for by in range(1, RING) for dc in range(CORES)] + [(0, 0, 1)]
-    for axis, by, dc in peers:
-        pl.semaphore_signal(barrier, inc=1, device_id=shifted(axis, by, (core + dc) % CORES), device_id_type=MESH)
-    row = lax.broadcasted_iota(jnp.int32, (t, t), 0)
-    col = lax.broadcasted_iota(jnp.int32, (t, t), 1)
-    upper[...] = jnp.where(row <= col, 1.0, 0.0).astype(bf16)
-    pl.semaphore_wait(barrier, len(peers))
-
-    told = []
-    for axis in range(3):
-        for by in range(1, RING):
-            told.append(remote(info_ref, info.at[axis, me[axis]], isend.at[axis, by], irecv.at[axis, by], shifted(axis, by)))
-            told[-1].start()
-
-    for load in mine + loads[:3]:
+    for axis, by, dc in PEERS:
+        pl.semaphore_signal(ready, inc=1, device_id=shifted(axis, by, (core + dc) % CORES), device_id_type=MESH)
+    xload = pltpu.make_async_copy(x_ref, xv, xload_sem)
+    xload.start()
+    for load in weight_loads:
         load.wait()
 
     def first(step):
@@ -372,6 +341,10 @@
             hh[:, at] = (a1 * (1.0 / (1.0 + jnp.exp(-a1))) * a3).astype(bf16)
             code(step - 1, codes * n // ups, codes * (n + 1) // ups)
 
+        @pl.when(step == 1)
+        def _():
+            pl.semaphore_wait(ready, len(PEERS))
+
         @pl.when(step > 0)
         def _():
             leave(step - 1)
@@ -472,8 +445,6 @@
     for k3 in LINES[:-1]:
         rest_of(k3)
 
-    for copy in told:
-        copy.wait_recv()
     for copy in moved:
         copy.wait_recv()
 
@@ -594,8 +565,8 @@
 
     lax.fori_loop(0, RING, line, 0)
 
-    loads[3].wait()
-    for g in everyone:
+    xload.wait()
+    for g in reversed(everyone):
         for way in range(2):
             home(g, way).wait_recv()
 
@@ -608,7 +579,7 @@
 
         lax.fori_loop(0, width[g] // 128, finish, 0)
 
-    for copy in told + hints + moved + later:
+    for copy in hints + moved + later:
         copy.wait_send()
 
     def last(step, _):
@@ -627,52 +598,85 @@
             home(g, way).wait_send()
 
 
-def experts(x, ids, gates, rx, w1, w3, w2):
+def layer_kernel(t, cap, groups, ids_ref, gates_ref, x_ref, w1_ref, w3_ref, w2_ref, y_ref, rx_ref, r2,
+                 w1, w3, w2, idv, gatev, info, upper, ready, small_sem, wsem, load_sem, gsend, grecv, rsend, rrecv, self_sem,
+                 isend, irecv, xload_sem, *sems):
+    hd, ff = w1.shape
+    n = len(groups)
+    wide = max(w for _, w in groups)
+    more = max(wide - min(w for _, w in groups), 128)
+    small = [pltpu.make_async_copy(a, b, small_sem.at[k]) for k, (a, b) in enumerate(((ids_ref, idv), (gates_ref, gatev)))]
+    weight_loads = [pltpu.make_async_copy(a, b, wsem.at[k])
+                    for k, (a, b) in enumerate(((w1_ref, w1), (w3_ref, w3), (w2_ref, w2)))]
+    for load in small:
+        load.start()
+    for load in small:
+        load.wait()
+
+    def there(got, out, pick):
+        dispatch_part(t, cap, groups, x_ref, rx_ref, idv, gatev, upper, info, load_sem, gsend, grecv, rsend, rrecv, self_sem,
+                      isend, irecv, weight_loads, got, out, pick)
+
+    pl.run_scoped(there,
+                  pltpu.VMEM((n, RING, RING, t + IDROWS, wide), bf16),
+                  pltpu.VMEM((n, RING, LINE, RING, cap, wide), bf16),
+                  pltpu.VMEM((LINE * cap, t), bf16))
+
+    def back(*scratch):
+        experts_part(t, cap, groups, x_ref, rx_ref, y_ref, r2, w1, w3, w2, info, upper, ready, weight_loads, xload_sem, sems,
+                     *scratch)
+
+    pl.run_scoped(back,
+                  pltpu.VMEM((2, RING, CORES, cap, hd), bf16),
+                  pltpu.VMEM((LINE * cap, ff), bf16),
+                  pltpu.VMEM((LINE * cap, hd), f32),
+                  pltpu.VMEM((LINE * cap, 128), f32),
+                  pltpu.VMEM((SLOTS, RING, CORES, cap, hd), i16),
+                  pltpu.VMEM((RING, RING, RING, CORES, cap, more), i16),
+                  pltpu.VMEM((RING, RING, RING, CORES, 1, 128), f32),
+                  pltpu.VMEM((n, LINE, RING, RING, cap, wide), i16),
+                  pltpu.VMEM((n, LINE, RING, RING, 1, 128), f32),
+                  pltpu.VMEM((n, RING, LINE, RING, 1, 128), f32),
+                  pltpu.VMEM((n, RING, t, wide), f32),
+                  pltpu.VMEM((n, 2, t // 2, wide), f32),
+                  pltpu.VMEM((n, 2, t, wide), f32),
+                  pltpu.VMEM((n, LINE, cap, wide), i16),
+                  pltpu.VMEM((LINE * cap, 3 * t), bf16),
+                  pltpu.VMEM((t, hd), bf16))
+
+
+def layer(x, ids, gates, w1, w3, w2, cap):
     t, hd = x.shape
     ff = w1.shape[1]
-    cap = rx.shape[4]
     groups = column_groups(hd, 128)
     wide = max(w for _, w in groups)
     n = len(groups)
-    more = max(wide - min(w for _, w in groups), 128)
-    info = jnp.concatenate([ids.T.astype(f32), gates.T], axis=0)
     dma = pltpu.SemaphoreType.DMA
     anywhere = pl.BlockSpec(memory_space=pl.ANY)
-    vmem = pl.BlockSpec(memory_space=pltpu.VMEM)
-    y, _ = pl.pallas_call(
-        functools.partial(experts_kernel, t, cap, groups),
+    y, _, _ = pl.pallas_call(
+        functools.partial(layer_kernel, t, cap, groups),
         out_shape=(jax.ShapeDtypeStruct((t, hd), bf16),
+                   jax.ShapeDtypeStruct((RING, RING, RING, CORES, cap, hd), bf16),
                    jax.ShapeDtypeStruct((n, RING, RING, LINE, cap, wide), i16)),
         in_specs=[anywhere] * 6,
-        out_specs=(vmem, anywhere),
+        out_specs=(pl.BlockSpec(memory_space=pltpu.VMEM), anywhere, anywhere),
         scratch_shapes=[
             pltpu.VMEM((hd, ff), bf16), pltpu.VMEM((hd, ff), bf16), pltpu.VMEM((ff, hd), bf16),
-            pltpu.VMEM((2, RING, CORES, cap, hd), bf16),
-            pltpu.VMEM((LINE * cap, ff), bf16),
-            pltpu.VMEM((LINE * cap, hd), f32),
-            pltpu.VMEM((LINE * cap, 128), f32),
-            pltpu.VMEM((SLOTS, RING, CORES, cap, hd), i16),
-            pltpu.VMEM((RING, RING, RING, CORES, cap, more), i16),
-            pltpu.VMEM((RING, RING, RING, CORES, 1, 128), f32),
-            pltpu.VMEM((n, LINE, RING, RING, cap, wide), i16),
-            pltpu.VMEM((n, LINE, RING, RING, 1, 128), f32),
-            pltpu.VMEM((n, RING, LINE, RING, 1, 128), f32),
-            pltpu.VMEM((n, RING, t, wide), f32),
-            pltpu.VMEM((n, 2, t // 2, wide), f32),
-            pltpu.VMEM((n, 2, t, wide), f32),
-            pltpu.VMEM((3, RING, 16, t), f32),
-            pltpu.VMEM((n, LINE, cap, wide), i16),
-            pltpu.VMEM((LINE * cap, 3 * t), bf16),
+            pltpu.VMEM((IDROWS, t), jnp.int32), pltpu.VMEM((IDROWS, t), f32),
+            pltpu.VMEM((3, RING, 2 * IDROWS, t), f32),
             pltpu.VMEM((t, t), bf16),
-            pltpu.VMEM((t, hd), bf16),
-            dma((4,)), dma((2,)), dma((3, RING)), dma((3, RING)),
-            dma((SLOTS, LINE + 4)), dma((n, LINE)), dma((n, LINE)), dma((n, LINE)),
+            pltpu.SemaphoreType.REGULAR,
+            dma((2,)), dma((3,)), dma((n,)),
+            dma((n, 4 + 4 * RING)), dma((n, 4 + 4 * RING)), dma((n, RING, LINE)), dma((n, RING, LINE)), dma((n, RING)),
+            dma((3, RING)), dma((3, RING)), dma,
+            dma((2,)), dma((SLOTS, LINE + 4)), dma((n, LINE)), dma((n, LINE)), dma((n, LINE)),
             dma((n, RING, RING)), dma((n, RING, RING)), dma((n, RING)), dma((n, RING)),
-            dma((n, 2)), dma((n, 2)), dma((n, 2)), dma((n, 2)), dma((LINE,)), dma((LINE,)), dma((RING, RING)), dma((RING, RING)), dma((n,)),
+            dma((n, 2)), dma((n, 2)), dma((n, 2)), dma((n, 2)), dma((LINE,)), dma((LINE,)),
+            dma((RING, RING)), dma((RING, RING)), dma((n,)),
         ],
-        compiler_params=pltpu.CompilerParams(collective_id=1, has_side_effects=True, vmem_limit_bytes=67043328),
-        name="experts",
-    )(info, x, rx, w1, w3, w2)
+        compiler_params=pltpu.CompilerParams(collective_id=0, has_side_effects=True, vmem_limit_bytes=67043328),
+        name="layer",
+    )(ids.T, gates.T, x, w1, w3, w2)
     return y
 
 
@@ -684,8 +688,7 @@
     def local(x, ids, gates, w1, w3, w2):
         t = x.shape[0]
         cap = min(t, CAPF * t * ids.shape[1] // nd)
-        rx = dispatch(x, ids, cap)
-        return experts(x, ids, gates, rx, w1[0], w3[0], w2[0])
+        return layer(x, ids, gates, w1[0], w3[0], w2[0], cap)
 
     return jax.shard_map(local, mesh=mesh, in_specs=(tok, tok, tok, wsp, wsp, wsp),
                          out_specs=tok, check_vma=False)

time: 313 us -> 308 us (0.984)
    pallas_call x2 -> x1, Pallas kernels: 308 us -> 305 us  [layer(): pl.pallas_call(functools.partial(layer_kernel, t, cap, groups), out_shape...]
where the time goes in v7:
time: 308 us; the launch traced here: 307 us
  Pallas kernels  305 us (99%)
    pallas_call x1, Pallas kernels, layer(): pl.pallas_call(functools.partial(layer_kernel, t, cap, groups), out_shape...  305 us

profile of v7, /device:TPU:1, one launch (start us, length us, event | category | flops | bytes accessed | tf_op | source)
XLA Modules:
  0.0 307.3 jit_solution(1289522618421872054)
XLA Ops:
  0.0 305.0 %layer.1 = (bf16[256,2048]{1,0:T(8,128)(2,1)}, bf16[4,4,4,2,32,2048]{5,4,3,2,1,0:T(8,128)(2,1)}, s16[3,4,4,8,32,768]{5,4,3,2,1,0:T(8,128)(2,1)}) custom-call(s32[8,256]{1,0:T(8,128)} %bitcast.8, f32[8,256]{1,0:T(8,128)} %bitcast.9, bf16[256,2048]{1,0:T(8,128)(2,1)} %x_ref.1, bf16[2048,768]{1,0:T(8,128)(2,1)} %bitcast.5, bf16[2048,768]{1,0:T(8,128)(2,1)} %bitcast.6, ...), custom_call_target="tpu_custom_call" | custom-call | tf_op jit(solution)/shard_map/layer/pallas_call | solution.py:656
  305.0 2.3 copy.8

commit v8 on v7

--- a/solution.py
+++ b/solution.py
@@ -19,6 +19,7 @@
 TILE = 256
 LINES = (2, 1, 3, 0)
 WIDE = 512
+PIECE = 256
 SLOTS = 5
 MESH = pl.DeviceIdType.MESH
 PEERS = [(axis, by, dc) for axis in range(3) for by in range(1, RING) for dc in range(CORES)] + [(0, 0, 1)]
@@ -108,6 +109,14 @@
         second(g, 0)
     for load in weight_loads:
         load.start()
+    told = []
+    for axis in range(3):
+        for by in range(1, RING):
+            told.append(pltpu.make_async_remote_copy(
+                src_ref=info.at[axis, me[axis]], dst_ref=info.at[axis, me[axis]], send_sem=isend.at[axis, by],
+                recv_sem=irecv.at[axis, by], device_id=shifted(axis, by), device_id_type=MESH))
+            told[-1].start()
+
     for g in everyone:
         p = ORDERS[g][0]
         hops[g, 0].wait_recv()
@@ -202,14 +211,6 @@
             hops[g, 7 + 4 * i].wait_recv()
         choose(g, 2)
         exchange(g, 2)
-
-    told = []
-    for axis in range(3):
-        for by in range(1, RING):
-            told.append(pltpu.make_async_remote_copy(
-                src_ref=info.at[axis, me[axis]], dst_ref=info.at[axis, me[axis]], send_sem=isend.at[axis, by],
-                recv_sem=irecv.at[axis, by], device_id=shifted(axis, by), device_id_type=MESH))
-            told[-1].start()
 
     for copy in sends:
         copy.wait_recv()
@@ -452,28 +453,31 @@
 
     def weights(g, h3, src):
         first_axis, axis, third = RETURNS[g]
-        ids = info[third, h3, 0:8, :]
-        gates = info[third, h3, 8:16, :]
         base = src * STRIDES[axis] + me[third] * STRIDES[third]
-        hits, gate = [], []
-        for k in range(LINE):
-            same = ids == (base + (k // CORES) * STRIDES[first_axis] + k % CORES).astype(f32)
-            hits.append(jnp.sum(jnp.where(same, 1.0, 0.0), axis=0, keepdims=True))
-            gate.append(jnp.sum(jnp.where(same, gates, 0.0), axis=0, keepdims=True))
-        hit = jnp.concatenate(hits, axis=0)
-        rank = jnp.dot(hit.astype(bf16), upper[...], preferred_element_type=f32)
-        slot = jnp.where((hit > 0.5) & (rank < cap + 0.5), rank - 1.0, -1.0)
-        for k in range(LINE):
+        found = {}
+
+        def begin():
+            ids = info[third, h3, 0:8, :]
+            gates = info[third, h3, 8:16, :]
+            hits, gate = [], []
+            for k in range(LINE):
+                same = ids == (base + (k // CORES) * STRIDES[first_axis] + k % CORES).astype(f32)
+                hits.append(jnp.sum(jnp.where(same, 1.0, 0.0), axis=0, keepdims=True))
+                gate.append(jnp.sum(jnp.where(same, gates, 0.0), axis=0, keepdims=True))
+            hit = jnp.concatenate(hits, axis=0)
+            rank = jnp.dot(hit.astype(bf16), upper[...], preferred_element_type=f32)
+            found["slot"] = jnp.where((hit > 0.5) & (rank < cap + 0.5), rank - 1.0, -1.0)
+            found["gate"] = gate
+
+        def expert(k):
             scale = jnp.sum(jnp.where(eye, s2[g, src, k, h3], 0.0), axis=1, keepdims=True)
-            w = jnp.where(slot[k:k + 1, :] == wanted, gate[k], 0.0) * scale
-            a = w.astype(bf16)
-            w = w - a.astype(f32)
-            b = w.astype(bf16)
-            w = w - b.astype(f32)
-            at = pl.ds(k * cap, cap)
-            wt[at, pl.ds(0, t)] = a
-            wt[at, pl.ds(t, t)] = b
-            wt[at, pl.ds(2 * t, t)] = w.astype(bf16)
+            w = jnp.where(found["slot"][k:k + 1, :] == wanted, found["gate"][k], 0.0) * scale
+            for p in range(3):
+                a = w.astype(bf16)
+                wt[g, pl.ds(p * rows + k * cap, cap), :] = a
+                w = w - a.astype(f32)
+
+        return [begin] + [functools.partial(expert, k) for k in range(LINE)]
 
     def line(index, _):
         k3 = 2 - index + 3 * (index // 2) - 2 * (index // 3)
@@ -507,29 +511,37 @@
                         second_more(k3, d).wait_recv()
                     fetch(g).start()
 
+            @pl.when(turn > 0)
+            def _():
+                for g in everyone:
+                    fetch(g).wait()
+
+            def piece(g, begin, size):
+                at = pl.ds(begin, size)
+                q = db[g, :, :, at].reshape(rows, size).astype(f32)
+                high = q.astype(bf16)
+                low = (q - high.astype(f32)).astype(bf16)
+                dims = (((0,), (0,)), ((), ()))
+                p = (lax.dot_general(wt[g], jnp.concatenate([high] * 3, axis=0), dims, preferred_element_type=f32)
+                     + lax.dot_general(wt[g], jnp.concatenate([low] * 3, axis=0), dims, preferred_element_type=f32))
+                acc[g, index, :, at] += p
+
+            def steps_of(g):
+                _, axis, third = RETURNS[g]
+                return weights(g, (me[third] + k3) % RING, (me[axis] - d) % RING)
+
+            for act in steps_of(0):
+                act()
             for g in everyone:
-                _, axis, third = RETURNS[g]
-                weights(g, (me[third] + k3) % RING, (me[axis] - d) % RING)
-
-                @pl.when(turn > 0)
-                def _():
-                    fetch(g).wait()
-
-                def piece(at, size):
-                    q = db[g, :, :, at].reshape(rows, size).astype(f32)
-                    high = q.astype(bf16)
-                    low = (q - high.astype(f32)).astype(bf16)
-                    dims = (((0,), (0,)), ((), ()))
-                    p = (lax.dot_general(wt[...], high, dims, preferred_element_type=f32)
-                         + lax.dot_general(wt[...], low, dims, preferred_element_type=f32))
-                    acc[g, index, :, at] += p[0:t] + p[t:2 * t] + p[2 * t:]
-
-                begin = 0
-                while begin < width[g]:
-                    size = min(WIDE, width[g] - begin)
-                    piece(pl.ds(begin, size), size)
-                    begin += size
-
+                products = [functools.partial(piece, g, begin, min(PIECE, width[g] - begin))
+                            for begin in range(0, width[g], PIECE)]
+                others = steps_of(g + 1) if g + 1 < len(groups) else []
+                for k, act in enumerate(products):
+                    act()
+                    for other in others[len(others) * k // len(products):len(others) * (k + 1) // len(products)]:
+                        other()
+
+            for g in everyone:
                 @pl.when((turn == RING - 1) & (index == 0))
                 def _():
                     for way in range(2):
@@ -641,7 +653,7 @@
                   pltpu.VMEM((n, 2, t // 2, wide), f32),
                   pltpu.VMEM((n, 2, t, wide), f32),
                   pltpu.VMEM((n, LINE, cap, wide), i16),
-                  pltpu.VMEM((LINE * cap, 3 * t), bf16),
+                  pltpu.VMEM((n, 3 * LINE * cap, t), bf16),
                   pltpu.VMEM((t, hd), bf16))
 
 

time: 308 us -> 305 us (level)
  no operation moved by 1% of the time
where the time goes in v8:
time: 305 us
  Pallas kernels  303 us (99%)
    pallas_call x1, Pallas kernels, layer(): pl.pallas_call(functools.partial(layer_kernel, t, cap, groups), out_shape...  303 us

profile of v8, /device:TPU:1, one launch (start us, length us, event | category | flops | bytes accessed | tf_op | source)
XLA Modules:
  0.0 304.8 jit_solution(2822642591285723041)
XLA Ops:
  0.0 302.5 %layer.1 = (bf16[256,2048]{1,0:T(8,128)(2,1)}, bf16[4,4,4,2,32,2048]{5,4,3,2,1,0:T(8,128)(2,1)}, s16[3,4,4,8,32,768]{5,4,3,2,1,0:T(8,128)(2,1)}) custom-call(s32[8,256]{1,0:T(8,128)} %bitcast.8, f32[8,256]{1,0:T(8,128)} %bitcast.9, bf16[256,2048]{1,0:T(8,128)(2,1)} %x_ref.1, bf16[2048,768]{1,0:T(8,128)(2,1)} %bitcast.5, bf16[2048,768]{1,0:T(8,128)(2,1)} %bitcast.6, ...), custom_call_target="tpu_custom_call" | custom-call | tf_op jit(solution)/shard_map/layer/pallas_call | solution.py:668
  302.5 2.3 copy.8

commit v9 on v8

--- a/solution.py
+++ b/solution.py
@@ -35,8 +35,68 @@
     return list(zip(starts, widths))
 
 
+EARLY = 2
+
+
+def homes(step):
+    turn, k = step // RING, step % RING
+    dy = (1 + 2 * k - 3 * (k // 2)) % RING
+    return (dy + 2 - turn + 3 * (turn // 2) - 2 * (turn // 3)) % RING, dy
+
+
+def tile_load(step, me, rx_ref, xb, xsem):
+    dz, dy = homes(step)
+    return pltpu.make_async_copy(rx_ref.at[(me[0] + dz) % RING, (me[1] + dy) % RING], xb.at[step % 2], xsem.at[step % 2])
+
+
+def diagonal(cap):
+    return lax.broadcasted_iota(jnp.int32, (cap, 128), 0) == lax.broadcasted_iota(jnp.int32, (cap, 128), 1)
+
+
+def code(step, begin, end, res, top, ob):
+    slot = step % SLOTS
+    cap = ob.shape[3]
+    for n in range(begin, end):
+        at = pl.ds(n * 128, 128)
+        v = jnp.round(res[:, at] * top[...]).astype(jnp.int32).astype(i16)
+        ob[slot, :, :, :, at] = v.reshape(RING, CORES, cap, 128)
+
+
+def up(step, w1, w3, xb, hh, res, top, ob):
+    hd, ff = w1.shape
+    rows = hh.shape[0]
+    ups, codes = ff // TILE, hd // 128
+    for n in range(ups):
+        at = pl.ds(n * TILE, TILE)
+        xt = xb[step % 2].reshape(rows, hd)
+        a1 = jnp.dot(xt, w1[:, at], preferred_element_type=f32)
+        a3 = jnp.dot(xt, w3[:, at], preferred_element_type=f32)
+        hh[:, at] = (a1 * (1.0 / (1.0 + jnp.exp(-a1))) * a3).astype(bf16)
+        code(step - 1, codes * n // ups, codes * (n + 1) // ups, res, top, ob)
+
+
+def down(step, me, w2, hh, res, top, so):
+    ff, hd = w2.shape
+    rows = hh.shape[0]
+    cap = rows // LINE
+    dz, dy = homes(step)
+    zh, yh = (me[0] + dz) % RING, (me[1] + dy) % RING
+    most = jnp.zeros((rows, 128), f32)
+    for n in range(hd // WIDE):
+        o = jnp.dot(hh[...], w2[:, n * WIDE:(n + 1) * WIDE], preferred_element_type=f32)
+        res[:, n * WIDE:(n + 1) * WIDE] = o
+        o = jnp.abs(o)
+        for k in range(WIDE // 128):
+            most = jnp.maximum(most, o[:, k * 128:(k + 1) * 128])
+    peak = jnp.maximum(jnp.max(most, axis=1, keepdims=True), 1e-30)
+    top[...] = jnp.broadcast_to(FULL / peak, top.shape)
+    for k in range(LINE):
+        part = jnp.where(diagonal(cap), peak[k * cap:(k + 1) * cap], 0.0)
+        so[zh, yh, k // CORES, k % CORES] = jnp.sum(part, axis=0, keepdims=True) * (1.0 / FULL)
+
+
 def dispatch_part(t, cap, groups, x_ref, rx_ref, idv, gatev, upper, info, load_sem, gsend, grecv, rsend, rrecv, self_sem,
-                  isend, irecv, weight_loads, got, out, pick):
+                  isend, irecv, weight_loads, xsem, w1, w3, w2, xb, hh, res, top, ob, so, got, out, pick):
     ey, ex, dp = lax.axis_index("ey"), lax.axis_index("ex"), lax.axis_index("dp")
     me = [ey // RING, ey % RING, ex // CORES]
     core = ex % CORES
@@ -172,7 +232,7 @@
         at[r] = me[r]
         return ref.at[at[0], at[1], at[2], core, :, pl.ds(start, width)]
 
-    sends, keeps = [], []
+    sends = {}
 
     def exchange(g, j):
         _, _, r = ORDERS[g]
@@ -183,14 +243,13 @@
                 src = out.at[g, j, to * CORES + c, :, :, pl.ds(0, width)]
                 if dr == 0 and dc == 0:
                     copy = pltpu.make_async_copy(src, place_in(rx_ref, g, j), self_sem.at[g, j])
-                    keeps.append(copy)
                 else:
                     n = dr * CORES + dc
                     copy = pltpu.make_async_remote_copy(
                         src_ref=src, dst_ref=place_in(rx_ref, g, j),
                         send_sem=rsend.at[g, j, n], recv_sem=rrecv.at[g, j, n],
                         device_id=shifted(r, dr, c), device_id_type=MESH)
-                    sends.append(copy)
+                sends.setdefault((g, j), []).append(copy)
                 copy.start()
 
     for g in everyone:
@@ -205,28 +264,47 @@
         for g in everyone:
             choose(g, j)
             exchange(g, j)
-    for g in everyone:
+    for g in (2, 0, 1):
         for i in range(RING):
             hops[g, 6 + 4 * i].wait_recv()
             hops[g, 7 + 4 * i].wait_recv()
         choose(g, 2)
         exchange(g, 2)
 
-    for copy in sends:
-        copy.wait_recv()
-    for copy in keeps:
-        copy.wait()
-    for copy in hops.values():
-        copy.wait_send()
-    for copy in sends + told:
+    def arrived(which):
+        for each in which:
+            for copy in sends[each][1:]:
+                copy.wait_recv()
+            sends[each][0].wait()
+
+    last = [(0, 2), (1, 2)]
+    arrived([each for each in sends if each not in last])
+    for load in weight_loads:
+        load.wait()
+    tile_load(0, me, rx_ref, xb, xsem).start()
+
+    def tile(step, _):
+        @pl.when(step + 1 < EARLY)
+        def _():
+            tile_load(step + 1, me, rx_ref, xb, xsem).start()
+
+        tile_load(step, me, rx_ref, xb, xsem).wait()
+        up(step, w1, w3, xb, hh, res, top, ob)
+        down(step, me, w2, hh, res, top, so)
+        return 0
+
+    lax.fori_loop(0, EARLY, tile, 0)
+
+    arrived(last)
+    for copy in list(hops.values()) + told + [copy for each in sends.values() for copy in each[1:]]:
         copy.wait_send()
     for copy in told:
         copy.wait_recv()
 
 
-def experts_part(t, cap, groups, x_ref, rx_ref, y_ref, r2, w1, w3, w2, info, upper, ready, weight_loads, xload_sem, sems,
-                 xb, hh, res, top, ob, rest, so, r1, s1, s2, acc, part, planes, db, wt, xv):
-    xsem, p1s, p1r, q1s, q1r, p2s, p2r, q2s, q2r, p3s, p3r, hs, hr, e1s, e1r, e2s, e2r, dsem = sems
+def experts_part(t, cap, groups, x_ref, rx_ref, y_ref, r2, w1, w3, w2, info, upper, ready, ysem, xsem, sems,
+                 xb, hh, res, top, ob, so, yv, rest, r1, s1, s2, acc, part, planes, db, wt, xv):
+    p1s, p1r, q1s, q1r, p2s, p2r, q2s, q2r, p3s, p3r, hs, hr, e1s, e1r, e2s, e2r, dsem = sems
     ey, ex, dp = lax.axis_index("ey"), lax.axis_index("ex"), lax.axis_index("dp")
     me = [ey // RING, ey % RING, ex // CORES]
     core = ex % CORES
@@ -248,22 +326,11 @@
         return pltpu.make_async_remote_copy(src_ref=src, dst_ref=dst, send_sem=send, recv_sem=recv,
                                             device_id=to, device_id_type=MESH)
 
-    def homes(step):
-        left = RING * RING - 1 - step
-        return (left + left // RING) % RING, left % RING
-
-    def tile_load(step):
-        dz, dy = homes(step)
-        return pltpu.make_async_copy(rx_ref.at[(me[0] + dz) % RING, (me[1] + dy) % RING], xb.at[step % 2], xsem.at[step % 2])
-
-    tile_load(0).start()
-
     for axis, by, dc in PEERS:
         pl.semaphore_signal(ready, inc=1, device_id=shifted(axis, by, (core + dc) % CORES), device_id_type=MESH)
-    xload = pltpu.make_async_copy(x_ref, xv, xload_sem)
+    tile_load(EARLY, me, rx_ref, xb, xsem).start()
+    xload = pltpu.make_async_copy(x_ref, xv, ysem.at[len(groups)])
     xload.start()
-    for load in weight_loads:
-        load.wait()
 
     def first(step):
         dz, dy = homes(step)
@@ -295,14 +362,7 @@
                 def _():
                     act(copy)
 
-    eye = lax.broadcasted_iota(jnp.int32, (cap, 128), 0) == lax.broadcasted_iota(jnp.int32, (cap, 128), 1)
-
-    def code(step, begin, end):
-        slot = step % SLOTS
-        for n in range(begin, end):
-            at = pl.ds(n * 128, 128)
-            v = jnp.round(res[:, at] * top[...]).astype(jnp.int32).astype(i16)
-            ob[slot, :, :, :, at] = v.reshape(RING, CORES, cap, 128)
+    eye = diagonal(cap)
 
     def room(step):
         @pl.when(step >= SLOTS)
@@ -324,50 +384,28 @@
                     r1[g, own[g], lead, xh, :, pl.ds(0, width[g])] = ob[slot, xh, core, :, pl.ds(col0[g], width[g])]
 
     def tile(step, _):
-        dz, dy = homes(step)
-        zh, yh = (me[0] + dz) % RING, (me[1] + dy) % RING
-
         @pl.when(step + 1 < RING * RING)
         def _():
-            tile_load(step + 1).start()
+            tile_load(step + 1, me, rx_ref, xb, xsem).start()
 
         room(step - 1)
-        tile_load(step).wait()
-        ups, codes = ff // TILE, hd // 128
-        for n in range(ups):
-            at = pl.ds(n * TILE, TILE)
-            xt = xb[step % 2].reshape(rows, hd)
-            a1 = jnp.dot(xt, w1[:, at], preferred_element_type=f32)
-            a3 = jnp.dot(xt, w3[:, at], preferred_element_type=f32)
-            hh[:, at] = (a1 * (1.0 / (1.0 + jnp.exp(-a1))) * a3).astype(bf16)
-            code(step - 1, codes * n // ups, codes * (n + 1) // ups)
-
-        @pl.when(step == 1)
-        def _():
-            pl.semaphore_wait(ready, len(PEERS))
-
-        @pl.when(step > 0)
-        def _():
-            leave(step - 1)
-
-        most = jnp.zeros((rows, 128), f32)
-        for n in range(hd // WIDE):
-            o = jnp.dot(hh[...], w2[:, n * WIDE:(n + 1) * WIDE], preferred_element_type=f32)
-            res[:, n * WIDE:(n + 1) * WIDE] = o
-            o = jnp.abs(o)
-            for k in range(WIDE // 128):
-                most = jnp.maximum(most, o[:, k * 128:(k + 1) * 128])
-        peak = jnp.maximum(jnp.max(most, axis=1, keepdims=True), 1e-30)
-        top[...] = jnp.broadcast_to(FULL / peak, top.shape)
-        for k in range(LINE):
-            part = jnp.where(eye, peak[k * cap:(k + 1) * cap], 0.0)
-            so[zh, yh, k // CORES, k % CORES] = jnp.sum(part, axis=0, keepdims=True) * (1.0 / FULL)
+        tile_load(step, me, rx_ref, xb, xsem).wait()
+        up(step, w1, w3, xb, hh, res, top, ob)
+        leave(step - 1)
+        down(step, me, w2, hh, res, top, so)
         return 0
 
     steps = RING * RING
-    lax.fori_loop(0, steps, tile, 0)
+    pl.semaphore_wait(ready, len(PEERS))
+
+    def leave_early(step, _):
+        leave(step)
+        return 0
+
+    lax.fori_loop(0, EARLY - 1, leave_early, 0)
+    lax.fori_loop(EARLY, steps, tile, 0)
     room(steps - 1)
-    code(steps - 1, 0, hd // 128)
+    code(steps - 1, 0, hd // 128, res, top, ob)
     leave(steps - 1)
 
     def scales(g, coord, c):
@@ -577,20 +615,6 @@
 
     lax.fori_loop(0, RING, line, 0)
 
-    xload.wait()
-    for g in reversed(everyone):
-        for way in range(2):
-            home(g, way).wait_recv()
-
-        def finish(n, _):
-            at = pl.ds(pl.multiple_of(n * 128, 128), 128)
-            to = pl.ds(pl.multiple_of(col0[g] + n * 128, 128), 128)
-            total = acc[g, RING - 1, :, at] + planes[g, 0, :, at] + planes[g, 1, :, at]
-            y_ref[:, to] = (xv[:, to].astype(f32) + total).astype(bf16)
-            return 0
-
-        lax.fori_loop(0, width[g] // 128, finish, 0)
-
     for copy in hints + moved + later:
         copy.wait_send()
 
@@ -607,13 +631,36 @@
                     second_more(k3, d).wait_send()
         for way in range(2):
             opposite(g, way).wait_send()
+
+    xload.wait()
+    stores = []
+    for g in reversed(everyone):
+        for way in range(2):
+            home(g, way).wait_recv()
+
+        def finish(n, _):
+            at = pl.ds(pl.multiple_of(n * 128, 128), 128)
+            to = pl.ds(pl.multiple_of(col0[g] + n * 128, 128), 128)
+            total = acc[g, RING - 1, :, at] + planes[g, 0, :, at] + planes[g, 1, :, at]
+            yv[:, to] = (xv[:, to].astype(f32) + total).astype(bf16)
+            return 0
+
+        lax.fori_loop(0, width[g] // 128, finish, 0)
+        at = pl.ds(col0[g], width[g])
+        stores.append(pltpu.make_async_copy(yv.at[:, at], y_ref.at[:, at], ysem.at[g]))
+        stores[-1].start()
+
+    for g in everyone:
+        for way in range(2):
             home(g, way).wait_send()
+    for store in stores:
+        store.wait()
 
 
 def layer_kernel(t, cap, groups, ids_ref, gates_ref, x_ref, w1_ref, w3_ref, w2_ref, y_ref, rx_ref, r2,
-                 w1, w3, w2, idv, gatev, info, upper, ready, small_sem, wsem, load_sem, gsend, grecv, rsend, rrecv, self_sem,
-                 isend, irecv, xload_sem, *sems):
-    hd, ff = w1.shape
+                 w1, w3, w2, idv, gatev, info, upper, xb, hh, res, top, ob, so, yv, ready, small_sem, wsem, load_sem,
+                 gsend, grecv, rsend, rrecv, self_sem, isend, irecv, ysem, xsem, *sems):
+    hd = w1.shape[0]
     n = len(groups)
     wide = max(w for _, w in groups)
     more = max(wide - min(w for _, w in groups), 128)
@@ -627,7 +674,7 @@
 
     def there(got, out, pick):
         dispatch_part(t, cap, groups, x_ref, rx_ref, idv, gatev, upper, info, load_sem, gsend, grecv, rsend, rrecv, self_sem,
-                      isend, irecv, weight_loads, got, out, pick)
+                      isend, irecv, weight_loads, xsem, w1, w3, w2, xb, hh, res, top, ob, so, got, out, pick)
 
     pl.run_scoped(there,
                   pltpu.VMEM((n, RING, RING, t + IDROWS, wide), bf16),
@@ -635,17 +682,11 @@
                   pltpu.VMEM((LINE * cap, t), bf16))
 
     def back(*scratch):
-        experts_part(t, cap, groups, x_ref, rx_ref, y_ref, r2, w1, w3, w2, info, upper, ready, weight_loads, xload_sem, sems,
-                     *scratch)
+        experts_part(t, cap, groups, x_ref, rx_ref, y_ref, r2, w1, w3, w2, info, upper, ready, ysem, xsem, sems,
+                     xb, hh, res, top, ob, so, yv, *scratch)
 
     pl.run_scoped(back,
-                  pltpu.VMEM((2, RING, CORES, cap, hd), bf16),
-                  pltpu.VMEM((LINE * cap, ff), bf16),
-                  pltpu.VMEM((LINE * cap, hd), f32),
-                  pltpu.VMEM((LINE * cap, 128), f32),
-                  pltpu.VMEM((SLOTS, RING, CORES, cap, hd), i16),
                   pltpu.VMEM((RING, RING, RING, CORES, cap, more), i16),
-                  pltpu.VMEM((RING, RING, RING, CORES, 1, 128), f32),
                   pltpu.VMEM((n, LINE, RING, RING, cap, wide), i16),
                   pltpu.VMEM((n, LINE, RING, RING, 1, 128), f32),
                   pltpu.VMEM((n, RING, LINE, RING, 1, 128), f32),
@@ -671,17 +712,24 @@
                    jax.ShapeDtypeStruct((RING, RING, RING, CORES, cap, hd), bf16),
                    jax.ShapeDtypeStruct((n, RING, RING, LINE, cap, wide), i16)),
         in_specs=[anywhere] * 6,
-        out_specs=(pl.BlockSpec(memory_space=pltpu.VMEM), anywhere, anywhere),
+        out_specs=(anywhere,) * 3,
         scratch_shapes=[
             pltpu.VMEM((hd, ff), bf16), pltpu.VMEM((hd, ff), bf16), pltpu.VMEM((ff, hd), bf16),
             pltpu.VMEM((IDROWS, t), jnp.int32), pltpu.VMEM((IDROWS, t), f32),
             pltpu.VMEM((3, RING, 2 * IDROWS, t), f32),
             pltpu.VMEM((t, t), bf16),
+            pltpu.VMEM((2, RING, CORES, cap, hd), bf16),
+            pltpu.VMEM((LINE * cap, ff), bf16),
+            pltpu.VMEM((LINE * cap, hd), f32),
+            pltpu.VMEM((LINE * cap, 128), f32),
+            pltpu.VMEM((SLOTS, RING, CORES, cap, hd), i16),
+            pltpu.VMEM((RING, RING, RING, CORES, 1, 128), f32),
+            pltpu.VMEM((t, hd), bf16),
             pltpu.SemaphoreType.REGULAR,
             dma((2,)), dma((3,)), dma((n,)),
             dma((n, 4 + 4 * RING)), dma((n, 4 + 4 * RING)), dma((n, RING, LINE)), dma((n, RING, LINE)), dma((n, RING)),
-            dma((3, RING)), dma((3, RING)), dma,
-            dma((2,)), dma((SLOTS, LINE + 4)), dma((n, LINE)), dma((n, LINE)), dma((n, LINE)),
+            dma((3, RING)), dma((3, RING)), dma((n + 1,)), dma((2,)),
+            dma((SLOTS, LINE + 4)), dma((n, LINE)), dma((n, LINE)), dma((n, LINE)),
             dma((n, RING, RING)), dma((n, RING, RING)), dma((n, RING)), dma((n, RING)),
             dma((n, 2)), dma((n, 2)), dma((n, 2)), dma((n, 2)), dma((LINE,)), dma((LINE,)),
             dma((RING, RING)), dma((RING, RING)), dma((n,)),

time: 305 us -> 302 us (level)
  Pallas kernels: 303 us -> 299 us
    pallas_call x1, Pallas kernels: 303 us -> 299 us  [layer(): pl.pallas_call(functools.partial(layer_kernel, t, cap, groups), out_shape...]
where the time goes in v9:
time: 302 us
  Pallas kernels  299 us (99%)
    pallas_call x1, Pallas kernels, layer(): pl.pallas_call(functools.partial(layer_kernel, t, cap, groups), out_shape...  299 us

profile of v9, /device:TPU:1, one launch (start us, length us, event | category | flops | bytes accessed | tf_op | source)
XLA Modules:
  0.0 301.6 jit_solution(8322291792548088360)
XLA Ops:
  0.0 299.3 %layer.1 = (bf16[256,2048]{1,0:T(8,128)(2,1)}, bf16[4,4,4,2,32,2048]{5,4,3,2,1,0:T(8,128)(2,1)}, s16[3,4,4,8,32,768]{5,4,3,2,1,0:T(8,128)(2,1)}) custom-call(s32[8,256]{1,0:T(8,128)} %bitcast.8, f32[8,256]{1,0:T(8,128)} %bitcast.9, bf16[256,2048]{1,0:T(8,128)(2,1)} %x_ref.1, bf16[2048,768]{1,0:T(8,128)(2,1)} %bitcast.5, bf16[2048,768]{1,0:T(8,128)(2,1)} %bitcast.6, ...), custom_call_target="tpu_custom_call" | custom-call | tf_op jit(solution)/shard_map/layer/pallas_call | solution.py:709
  299.3 2.3 copy.8

commit v10 on v9

--- a/solution.py
+++ b/solution.py
@@ -95,7 +95,7 @@
         so[zh, yh, k // CORES, k % CORES] = jnp.sum(part, axis=0, keepdims=True) * (1.0 / FULL)
 
 
-def dispatch_part(t, cap, groups, x_ref, rx_ref, idv, gatev, upper, info, load_sem, gsend, grecv, rsend, rrecv, self_sem,
+def dispatch_part(t, cap, groups, x_ref, rx_ref, small, idv, gatev, upper, info, load_sem, gsend, grecv, rsend, rrecv, self_sem,
                   isend, irecv, weight_loads, xsem, w1, w3, w2, xb, hh, res, top, ob, so, got, out, pick):
     ey, ex, dp = lax.axis_index("ey"), lax.axis_index("ex"), lax.axis_index("dp")
     me = [ey // RING, ey % RING, ex // CORES]
@@ -113,15 +113,17 @@
 
     loads = [pltpu.make_async_copy(x_ref.at[:, pl.ds(start, width)], got.at[g, 0, 0, pl.ds(0, t), pl.ds(0, width)],
                                    load_sem.at[g]) for g, (start, width) in enumerate(groups)]
-    for load in loads:
-        load.start()
 
     barrier = pltpu.get_barrier_semaphore()
     for axis, by, dc in PEERS:
         pl.semaphore_signal(barrier, inc=1, device_id=shifted(axis, by, (core + dc) % CORES), device_id_type=MESH)
+    for load in small + loads:
+        load.start()
     row = lax.broadcasted_iota(jnp.int32, (t, t), 0)
     col = lax.broadcasted_iota(jnp.int32, (t, t), 1)
     upper[...] = jnp.where(row <= col, 1.0, 0.0).astype(bf16)
+    for load in small:
+        load.wait()
     ids = idv[...].astype(f32)
     for g in range(len(groups)):
         got[g, 0, 0, pl.ds(t, IDROWS), pl.ds(0, t)] = ids.astype(bf16)
@@ -167,16 +169,6 @@
     for g in everyone:
         first(g)
         second(g, 0)
-    for load in weight_loads:
-        load.start()
-    told = []
-    for axis in range(3):
-        for by in range(1, RING):
-            told.append(pltpu.make_async_remote_copy(
-                src_ref=info.at[axis, me[axis]], dst_ref=info.at[axis, me[axis]], send_sem=isend.at[axis, by],
-                recv_sem=irecv.at[axis, by], device_id=shifted(axis, by), device_id_type=MESH))
-            told[-1].start()
-
     for g in everyone:
         p = ORDERS[g][0]
         hops[g, 0].wait_recv()
@@ -255,6 +247,15 @@
     for g in everyone:
         choose(g, 0)
         exchange(g, 0)
+    for load in weight_loads:
+        load.start()
+    told = []
+    for axis in range(3):
+        for by in range(1, RING):
+            told.append(pltpu.make_async_remote_copy(
+                src_ref=info.at[axis, me[axis]], dst_ref=info.at[axis, me[axis]], send_sem=isend.at[axis, by],
+                recv_sem=irecv.at[axis, by], device_id=shifted(axis, by), device_id_type=MESH))
+            told[-1].start()
     for i in (3, 1):
         for g in everyone:
             second_on(g, i)
@@ -667,13 +668,9 @@
     small = [pltpu.make_async_copy(a, b, small_sem.at[k]) for k, (a, b) in enumerate(((ids_ref, idv), (gates_ref, gatev)))]
     weight_loads = [pltpu.make_async_copy(a, b, wsem.at[k])
                     for k, (a, b) in enumerate(((w1_ref, w1), (w3_ref, w3), (w2_ref, w2)))]
-    for load in small:
-        load.start()
-    for load in small:
-        load.wait()
 
     def there(got, out, pick):
-        dispatch_part(t, cap, groups, x_ref, rx_ref, idv, gatev, upper, info, load_sem, gsend, grecv, rsend, rrecv, self_sem,
+        dispatch_part(t, cap, groups, x_ref, rx_ref, small, idv, gatev, upper, info, load_sem, gsend, grecv, rsend, rrecv, self_sem,
                       isend, irecv, weight_loads, xsem, w1, w3, w2, xb, hh, res, top, ob, so, got, out, pick)
 
     pl.run_scoped(there,

time: 302 us -> 301 us (level)
  no operation moved by 1% of the time
where the time goes in v10:
time: 301 us
  Pallas kernels  298 us (99%)
    pallas_call x1, Pallas kernels, layer(): pl.pallas_call(functools.partial(layer_kernel, t, cap, groups), out_shape...  298 us

profile of v10, /device:TPU:1, one launch (start us, length us, event | category | flops | bytes accessed | tf_op | source)
XLA Modules:
  0.0 300.8 jit_solution(11356144166534002058)
XLA Ops:
  0.0 298.5 %layer.1 = (bf16[256,2048]{1,0:T(8,128)(2,1)}, bf16[4,4,4,2,32,2048]{5,4,3,2,1,0:T(8,128)(2,1)}, s16[3,4,4,8,32,768]{5,4,3,2,1,0:T(8,128)(2,1)}) custom-call(s32[8,256]{1,0:T(8,128)} %bitcast.8, f32[8,256]{1,0:T(8,128)} %bitcast.9, bf16[256,2048]{1,0:T(8,128)(2,1)} %x_ref.1, bf16[2048,768]{1,0:T(8,128)(2,1)} %bitcast.5, bf16[2048,768]{1,0:T(8,128)(2,1)} %bitcast.6, ...), custom_call_target="tpu_custom_call" | custom-call | tf_op jit(solution)/shard_map/layer/pallas_call | solution.py:706
  298.5 2.3 copy.8

commit v11 on v10

--- a/solution.py
+++ b/solution.py
@@ -165,25 +165,6 @@
         hops[g, 5 + 4 * i].wait_recv()
         hop(g, 7 + 4 * i, (i, 1), (i, 2), q, 3, high)
 
-    everyone = range(len(groups))
-    for g in everyone:
-        first(g)
-        second(g, 0)
-    for g in everyone:
-        p = ORDERS[g][0]
-        hops[g, 0].wait_recv()
-        hop(g, 2, (3, 0), (2, 0), p, 1, low)
-        second(g, 3)
-        hops[g, 1].wait_recv()
-        hop(g, 3, (1, 0), (2, 0), p, 3, high)
-        second(g, 1)
-    for g in everyone:
-        second_on(g, 0)
-    for g in everyone:
-        hops[g, 2].wait_recv()
-        hops[g, 3].wait_recv()
-        second(g, 2)
-
     def choose(g, j):
         p, _, r = ORDERS[g]
         width = groups[g][1]
@@ -244,9 +225,27 @@
                 sends.setdefault((g, j), []).append(copy)
                 copy.start()
 
-    for g in everyone:
+    everyone = range(len(groups))
+    for g in everyone:
+        first(g)
+        second(g, 0)
+    for g in everyone:
+        p = ORDERS[g][0]
+        hops[g, 0].wait_recv()
+        hop(g, 2, (3, 0), (2, 0), p, 1, low)
+        second(g, 3)
+        hops[g, 1].wait_recv()
+        hop(g, 3, (1, 0), (2, 0), p, 3, high)
+        second(g, 1)
+    for g in everyone:
+        second_on(g, 0)
+    for g in everyone:
+        hops[g, 2].wait_recv()
+        hops[g, 3].wait_recv()
+        second(g, 2)
         choose(g, 0)
         exchange(g, 0)
+
     for load in weight_loads:
         load.start()
     told = []
@@ -451,7 +450,7 @@
         return remote(r1.at[0, :, h3, (me[axis] + d) % RING, :, at], r2.at[0, h3, me[axis], :, :, at],
                       e2s.at[k3, d], e2r.at[k3, d], shifted(axis, d))
 
-    for g in everyone:
+    for g in (1, 2, 0):
         axis = RETURNS[g][0]
         for n in range(1, LINE):
             d, dc = n // CORES, n % CORES

time: 301 us -> 302 us (level)
  no operation moved by 1% of the time
where the time goes in v11:
time: 302 us; the launch traced here: 301 us
  Pallas kernels  299 us (99%)
    pallas_call x1, Pallas kernels, layer(): pl.pallas_call(functools.partial(layer_kernel, t, cap, groups), out_shape...  299 us

profile of v11, /device:TPU:1, one launch (start us, length us, event | category | flops | bytes accessed | tf_op | source)
XLA Modules:
  0.0 301.5 jit_solution(14733924693649306450)
XLA Ops:
  0.0 299.1 %layer.1 = (bf16[256,2048]{1,0:T(8,128)(2,1)}, bf16[4,4,4,2,32,2048]{5,4,3,2,1,0:T(8,128)(2,1)}, s16[3,4,4,8,32,768]{5,4,3,2,1,0:T(8,128)(2,1)}) custom-call(s32[8,256]{1,0:T(8,128)} %bitcast.8, f32[8,256]{1,0:T(8,128)} %bitcast.9, bf16[256,2048]{1,0:T(8,128)(2,1)} %x_ref.1, bf16[2048,768]{1,0:T(8,128)(2,1)} %bitcast.5, bf16[2048,768]{1,0:T(8,128)(2,1)} %bitcast.6, ...), custom_call_target="tpu_custom_call" | custom-call | tf_op jit(solution)/shard_map/layer/pallas_call | solution.py:705
  299.2 2.3 copy.8

commit v12 on v10

--- a/solution.py
+++ b/solution.py
@@ -279,6 +279,10 @@
             sends[each][0].wait()
 
     last = [(0, 2), (1, 2)]
+    for copy in list(hops.values()) + told:
+        copy.wait_send()
+    for copy in told:
+        copy.wait_recv()
     arrived([each for each in sends if each not in last])
     for load in weight_loads:
         load.wait()
@@ -296,11 +300,14 @@
 
     lax.fori_loop(0, EARLY, tile, 0)
 
+    def gone(which):
+        for each in which:
+            for copy in sends[each][1:]:
+                copy.wait_send()
+
+    gone([each for each in sends if each[1] != 2])
     arrived(last)
-    for copy in list(hops.values()) + told + [copy for each in sends.values() for copy in each[1:]]:
-        copy.wait_send()
-    for copy in told:
-        copy.wait_recv()
+    gone([each for each in sends if each[1] == 2])
 
 
 def experts_part(t, cap, groups, x_ref, rx_ref, y_ref, r2, w1, w3, w2, info, upper, ready, ysem, xsem, sems,

time: 301 us -> 301 us (level)
  no operation moved by 1% of the time
where the time goes in v12:
time: 301 us
  Pallas kernels  298 us (99%)
    pallas_call x1, Pallas kernels, layer(): pl.pallas_call(functools.partial(layer_kernel, t, cap, groups), out_shape...  298 us

profile of v12, /device:TPU:1, one launch (start us, length us, event | category | flops | bytes accessed | tf_op | source)
XLA Modules:
  0.0 300.7 jit_solution(1847367313998610781)
XLA Ops:
  0.0 298.4 %layer.1 = (bf16[256,2048]{1,0:T(8,128)(2,1)}, bf16[4,4,4,2,32,2048]{5,4,3,2,1,0:T(8,128)(2,1)}, s16[3,4,4,8,32,768]{5,4,3,2,1,0:T(8,128)(2,1)}) custom-call(s32[8,256]{1,0:T(8,128)} %bitcast.8, f32[8,256]{1,0:T(8,128)} %bitcast.9, bf16[256,2048]{1,0:T(8,128)(2,1)} %x_ref.1, bf16[2048,768]{1,0:T(8,128)(2,1)} %bitcast.5, bf16[2048,768]{1,0:T(8,128)(2,1)} %bitcast.6, ...), custom_call_target="tpu_custom_call" | custom-call | tf_op jit(solution)/shard_map/layer/pallas_call | solution.py:713
  298.4 2.3 copy.8
